TPU v7x, 16 devices: a 4x2x1 block of a 4x4x8 slice. The times are simulated.
16 devices in a mesh: rep: 4 (over y, z, core), dp: 4 (over x).
Axes of the slice: x: 4, y: 2, z: 1, core: 2. Of those that a mesh axis runs over, the one named last changes fastest.
The devices are a block of a 4x4x8 slice.
Arguments:
- x: bfloat16 [16, 4096, 640], P(('rep', 'dp')), parts along dimension 0
- dy: bfloat16 [16, 4096, 640], P(('rep', 'dp')), parts along dimension 0
- w_gate: bfloat16 [2, 640, 2048], P(None, 'dp')
- w_up: bfloat16 [2, 640, 2048], P(None, 'dp')
- w_down: bfloat16 [2, 2048, 640], P(None, 'dp')
- m_w_gate: float32 [2, 640, 2048], P(None, 'dp')
- m_w_up: float32 [2, 640, 2048], P(None, 'dp')
- m_w_down: float32 [2, 2048, 640], P(None, 'dp')
- v_w_gate: float32 [2, 640, 2048], P(None, 'dp')
- v_w_up: float32 [2, 640, 2048], P(None, 'dp')
- v_w_down: float32 [2, 2048, 640], P(None, 'dp')
Outputs:
- output 1: bfloat16 [8, 640, 2048], P('rep', 'dp'), parts along dimension 0
- output 2: bfloat16 [8, 640, 2048], P('rep', 'dp'), parts along dimension 0
- output 3: bfloat16 [8, 2048, 640], P('rep', 'dp'), parts along dimension 0
- output 4: float32 [8, 640, 2048], P('rep', 'dp'), parts along dimension 0
- output 5: float32 [8, 640, 2048], P('rep', 'dp'), parts along dimension 0
- output 6: float32 [8, 2048, 640], P('rep', 'dp'), parts along dimension 0
- output 7: float32 [8, 640, 2048], P('rep', 'dp'), parts along dimension 0
- output 8: float32 [8, 640, 2048], P('rep', 'dp'), parts along dimension 0
- output 9: float32 [8, 2048, 640], P('rep', 'dp'), parts along dimension 0
There are 4 independent parts. A program takes and returns all parts, laid end to end along the dimension named above; an argument that names none is the same for every part.
All inputs are finite; a program needn't handle non-finite values.
Results may differ from a plain program's by a relative error of at most 0.022.
Values are sent between devices in bfloat16 or wider.
A program may use at most 768 MiB of HBM per device.

v0:
```python
import jax
import jax.numpy as jnp
from jax import lax
from jax.sharding import PartitionSpec as P

NAMES = ("w_gate", "w_up", "w_down")


def matmul(a, w):
    return jnp.dot(a, w, preferred_element_type=jnp.float32).astype(jnp.bfloat16)


def normed(h):
    wide = h.astype(jnp.float32)
    scale = lax.rsqrt(jnp.mean(wide**2, -1, keepdims=True) + 1e-6)
    return (wide * scale).astype(jnp.bfloat16)


def layer(h, w):
    a = normed(h)
    gate = jnp.dot(a, w["w_gate"], preferred_element_type=jnp.float32)
    up = jnp.dot(a, w["w_up"], preferred_element_type=jnp.float32)
    return h + matmul((jax.nn.silu(gate) * up).astype(jnp.bfloat16), w["w_down"])


def adamw(w, m, v, g):
    m = 0.9 * m + 0.1 * g
    v = 0.95 * v + 0.05 * g * g
    step = m * lax.rsqrt(v + 1e-8) + 0.1 * w
    return (w - 0.02 * step).astype(jnp.bfloat16), m, v


def clipped(gradients, sum_of_squares, count):
    factor = jnp.minimum(1.0, 0.5 * lax.rsqrt(sum_of_squares / count + 1e-30))
    return [g * factor for g in gradients]


def solution(mesh):
    def fetched(weights, number):
        return {name: lax.all_gather(w[number], "dp", axis=0, tiled=True) for name, w in zip(NAMES, weights, strict=True)}

    def step(x, dy, *arrays):
        weights, m, v = (arrays[i : i + 3] for i in (0, 3, 6))
        layers = weights[0].shape[0]
        h, kept = x[0], []
        for number in range(layers):
            kept.append(h)
            h = layer(h, fetched(weights, number))
        by_h, mine = dy[0], [None] * layers
        for number in reversed(range(layers)):
            _, back = jax.vjp(lambda w, h: layer(h, w), fetched(weights, number), kept[number])
            by_w, by_h = back(by_h)
            mine[number] = [lax.psum_scatter(by_w[name], "dp", scatter_dimension=0, tiled=True) for name in NAMES]
        gradients = [jnp.stack([mine[number][i] for number in range(layers)]).astype(jnp.float32) for i in range(3)]
        squares = lax.psum(sum(jnp.sum(g * g) for g in gradients), "dp")
        gradients = clipped(gradients, squares, lax.psum(1, "dp") * sum(g.size for g in gradients))
        new = [adamw(w.astype(jnp.float32), m, v, g) for w, m, v, g in zip(weights, m, v, gradients, strict=True)]
        return tuple(one[which] for which in range(3) for one in new)

    states, cut = P(("rep", "dp"), None, None), P(None, "dp", None)
    return jax.shard_map(
        step,
        mesh=mesh,
        in_specs=(states, states) + (cut,) * 9,
        out_specs=(P("rep", "dp", None),) * 9,
        check_vma=False,
    )
```

profile of v0, /device:TPU:112, one launch (start us, length us, event | category | flops | bytes accessed | tf_op | source)
XLA Modules:
  0.0 561.8 jit_solution(4114312962789967880)
XLA Ops:
  7.2 0.1 all-gather.13.cloned.1.call-start
  7.3 2.6 fusion.103
  9.8 0.1 all-gather.13.cloned.1.call-update
  9.9 0.1 all-gather.15.cloned.1.call-start
  10.0 2.5 fusion.102
  12.5 0.1 all-gather.15.cloned.1.call-update
  12.5 0.1 all-gather.17.cloned.1.call-start
  12.6 1.2 fusion.101
  13.8 0.1 all-gather.17.cloned.1.call-update
  13.8 0.1 all-gather.21.cloned.1.call-start
  13.9 0.6 all-gather.21.cloned.1.call-update
  14.5 0.1 all-gather.23.cloned.1.call-start
  14.5 0.6 all-gather.23.cloned.1.call-update
  15.1 0.1 all-gather.19.cloned.1.call-start
  15.2 0.6 all-gather.19.cloned.1.call-update
  15.8 0.1 reduce-scatter.15.cloned.1.call-start
  15.8 7.9 %copy.20 = bf16[1,4096,640]{1,2,0:T(8,128)(2,1)} copy(bf16[1,4096,640]{2,1,0:T(8,128)(2,1)} %param.11) | data formatting | bytes 10485760 | tf_op args[0]
  23.8 3.6 fusion.15
  27.4 7.9 %copy.21 = bf16[1,4096,640]{1,2,0:T(8,128)(2,1)} copy(bf16[1,4096,640]{2,1,0:T(8,128)(2,1)} %param.12) | data formatting | bytes 10485760 | tf_op args[1]
  35.3 8.5 %all-gather.13.cloned.1.call-done = bf16[1,640,2048]{2,1,0:T(8,128)(2,1)} async-done(((bf16[1,160,2048]{2,1,0:T(8,128)(2,1)}), bf16[1,640,2048]{2,1,0:T(8,128)(2,1)}) %all-gather.13.cloned.1.call-update) | async-done | bytes 2621456 | tf_op jit(solution)/shard_map/all_gather | solution.py:40
  43.8 21.8 %fusion.40 = f32[4096,2048]{1,0:T(8,128)} fusion(bf16[1,4096,640]{1,2,0:T(8,128)(2,1)} %copy.20, f32[4096]{0:T(1024)S(1)} %add_rsqrt_fusion, bf16[1,640,2048]{2,1,0:T(8,128)(2,1)} %all-gather.13.cloned.1.call-done), kind=kOutput, calls=%fused_computation.55 | convolution fusion | flops 10745282560 | bytes 41435136 | tf_op jit(solution)/shard_map/dot_general | solution.py:21
  65.6 11.3 %all-gather.15.cloned.1.call-done = bf16[1,640,2048]{2,1,0:T(8,128)(2,1)} async-done(((bf16[1,160,2048]{2,1,0:T(8,128)(2,1)}), bf16[1,640,2048]{2,1,0:T(8,128)(2,1)}) %all-gather.15.cloned.1.call-update) | async-done | bytes 2621456 | tf_op jit(solution)/shard_map/all_gather | solution.py:40
  76.9 34.0 %multiply_convert_fusion.1 = (bf16[4096,2048]{1,0:T(8,128)(2,1)}, f32[4096,2048]{1,0:T(8,128)}) fusion(f32[4096,2048]{1,0:T(8,128)} %fusion.40, bf16[1,640,2048]{2,1,0:T(8,128)(2,1)} %all-gather.15.cloned.1.call-done, bf16[1,4096,640]{1,2,0:T(8,128)(2,1)} %copy.20, f32[4096]{0:T(1024)S(1)} %add_rsqrt_fusion), kind=kOutput, calls=%fused_computation.17 | convolution fusion | flops 10795614208 | bytes 91766784 | tf_op jit(solution)/shard_map/dot_general | solution.py:22
  110.9 18.7 %fusion.19 = (f32[4096]{0:T(1024)S(1)}, bf16[4096,640]{0,1:T(8,128)(2,1)}) fusion(bf16[4096,2048]{1,0:T(8,128)(2,1)} %get-tuple-element.24, bf16[1,2048,640]{2,1,0:T(8,128)(2,1)} %all-gather.17.cloned.1.call-done, bf16[1,4096,640]{1,2,0:T(8,128)(2,1)} %copy.20), kind=kOutput, calls=%fused_computation.37 | convolution fusion | flops 10750521344 | bytes 29900800 | tf_op jit(solution)/shard_map/dot_general | solution.py:10
  129.6 13.3 %all-gather.21.cloned.1.call-done = bf16[1,2048,640]{2,1,0:T(8,128)(2,1)} async-done(((bf16[1,512,640]{2,1,0:T(8,128)(2,1)}), bf16[1,2048,640]{2,1,0:T(8,128)(2,1)}) %all-gather.21.cloned.1.call-update) | async-done | bytes 2621456 | tf_op jit(solution)/shard_map/all_gather | solution.py:40
  142.9 19.9 %convolution_convert_fusion.1 = bf16[4096,2048]{1,0:T(8,128)(2,1)} fusion(bf16[1,4096,640]{2,1,0:T(8,128)(2,1)} %param.12, bf16[1,2048,640]{2,1,0:T(8,128)(2,1)} %all-gather.21.cloned.1.call-done), kind=kOutput, calls=%fused_computation.29 | convolution fusion | flops 10745806848 | bytes 24641536 | tf_op jit(solution)/shard_map/transpose(jvp())/dot_general | solution.py:10
  162.8 13.1 %all-gather.23.cloned.1.call-done = bf16[1,640,2048]{2,1,0:T(8,128)(2,1)} async-done(((bf16[1,160,2048]{2,1,0:T(8,128)(2,1)}), bf16[1,640,2048]{2,1,0:T(8,128)(2,1)}) %all-gather.23.cloned.1.call-update) | async-done | bytes 2621456 | tf_op jit(solution)/shard_map/all_gather | solution.py:40
  175.8 21.8 %fusion.32 = f32[4096,2048]{1,0:T(8,128)} fusion(bf16[4096,640]{0,1:T(8,128)(2,1)} %get-tuple-element.27, f32[4096]{0:T(1024)S(1)} %fusion.89, bf16[1,640,2048]{2,1,0:T(8,128)(2,1)} %all-gather.23.cloned.1.call-done), kind=kOutput, calls=%fused_computation.52 | convolution fusion | flops 10745282560 | bytes 41435136 | tf_op jit(solution)/shard_map/jvp()/dot_general | solution.py:22
  197.6 11.2 %all-gather.19.cloned.1.call-done = bf16[1,640,2048]{2,1,0:T(8,128)(2,1)} async-done(((bf16[1,160,2048]{2,1,0:T(8,128)(2,1)}), bf16[1,640,2048]{2,1,0:T(8,128)(2,1)}) %all-gather.19.cloned.1.call-update) | async-done | bytes 2621456 | tf_op jit(solution)/shard_map/all_gather | solution.py:40
  208.8 44.8 %fusion.2 = (bf16[4096,2048]{1,0:T(8,128)(2,1)}, f32[4096,2048]{1,0:T(8,128)}) fusion(f32[4096,2048]{1,0:T(8,128)} %fusion.32, bf16[4096,2048]{1,0:T(8,128)(2,1)} %convolution_convert_fusion.1, bf16[1,640,2048]{2,1,0:T(8,128)(2,1)} %all-gather.19.cloned.1.call-done, bf16[4096,640]{0,1:T(8,128)(2,1)} %get-tuple-element.27, f32[4096]{0:T(1024)S(1)} %fusion.89), kind=kOutput, calls=%fused_computation.8 | convolution fusion | flops 10845945856 | bytes 108544000 | tf_op jit(solution)/shard_map/jvp()/dot_general | solution.py:21
  253.6 17.1 %convolution_convert_fusion.3 = bf16[4096,640]{0,1:T(8,128)(2,1)} fusion(bf16[4096,2048]{1,0:T(8,128)(2,1)} %get-tuple-element.28, bf16[1,640,2048]{2,1,0:T(8,128)(2,1)} %all-gather.19.cloned.1.call-done), kind=kOutput, calls=%fused_computation.42 | convolution fusion | flops 10737418240 | bytes 24641536 | tf_op jit(solution)/shard_map/transpose(jvp())/dot_general | solution.py:21
  270.7 25.6 %fusion.21 = (f32[4096]{0:T(1024)S(1)}, bf16[4096,640]{0,1:T(8,128)(2,1)}) fusion(bf16[4096,640]{0,1:T(8,128)(2,1)} %get-tuple-element.27, bf16[4096,640]{0,1:T(8,128)(2,1)} %convolution_convert_fusion.3, bf16[1,640,2048]{2,1,0:T(8,128)(2,1)S(1)} %copy-done.19, bf16[4096,2048]{1,0:T(8,128)(2,1)} %convolution_convert_fusion.1, ...), kind=kOutput, calls=%fused_computation.39 | convolution fusion | flops 10803474432 | bytes 68698112 | tf_op jit(solution)/shard_map/transpose(jvp())/dot_general | solution.py:22
  296.2 11.9 %fusion.26 = bf16[4096,640]{0,1:T(8,128)(2,1)} fusion(bf16[4096,640]{0,1:T(8,128)(2,1)} %get-tuple-element.27, bf16[4096,640]{0,1:T(8,128)(2,1)} %get-tuple-element.31, bf16[1,4096,640]{1,2,0:T(8,128)(2,1)} %copy.21, f32[4096]{0:T(1024)S(1)} %multiply_multiply_fusion.3, f32[4096]{0:T(1024)S(1)} %fusion.89), kind=kLoop, calls=%fused_computation.45 | loop fusion | flops 18350080 | bytes 21004288 | tf_op jit(solution)/shard_map/transpose(jvp())/add_any | solution.py:14
  308.2 19.6 %convolution_convert_fusion.4 = bf16[2048,640]{1,0:T(8,128)(2,1)} fusion(bf16[4096,2048]{1,0:T(8,128)(2,1)} %get-tuple-element.24, bf16[4096,640]{0,1:T(8,128)(2,1)} %fusion.26), kind=kOutput, calls=%fused_computation.71 | convolution fusion | flops 10738728960 | bytes 24641536 | tf_op jit(solution)/shard_map/transpose(jvp())/dot_general | solution.py:10
  327.7 0.1 reduce-scatter.15.cloned.1.call-update
  327.8 0.1 reduce-scatter.17.cloned.1.call-start
  327.9 27.2 %fusion.45 = bf16[2048,640]{1,0:T(8,128)(2,1)} fusion(bf16[1,4096,640]{2,1,0:T(8,128)(2,1)} %param.12, f32[4096,2048]{1,0:T(8,128)} %fusion.32, f32[4096,2048]{1,0:T(8,128)} %get-tuple-element.29), kind=kOutput, calls=%fused_computation.69 | convolution fusion | flops 10789060608 | bytes 74973184 | tf_op jit(solution)/shard_map/transpose(jvp())/dot_general | solution.py:10
  355.1 0.1 reduce-scatter.17.cloned.1.call-update
  355.1 0.1 reduce-scatter.11.cloned.1.call-start
  355.2 18.8 %convolution_convert_fusion = bf16[4096,2048]{1,0:T(8,128)(2,1)} fusion(bf16[4096,640]{0,1:T(8,128)(2,1)} %fusion.26, bf16[1,2048,640]{2,1,0:T(8,128)(2,1)S(1)} %copy-done.18), kind=kOutput, calls=%fused_computation.28 | convolution fusion | flops 10745806848 | bytes 24641536 | tf_op jit(solution)/shard_map/transpose(jvp())/dot_general | solution.py:10
  374.0 22.4 %fusion.56 = bf16[640,2048]{1,0:T(8,128)(2,1)} fusion(bf16[4096,2048]{1,0:T(8,128)(2,1)} %convolution_convert_fusion, f32[4096,2048]{1,0:T(8,128)} %fusion.40, bf16[1,4096,640]{1,2,0:T(8,128)(2,1)} %copy.20, f32[4096]{0:T(1024)S(1)} %copy-done.17), kind=kOutput, calls=%fused_computation.73 | convolution fusion | flops 10796924928 | bytes 58212352 | tf_op jit(solution)/shard_map/transpose(jvp())/dot_general | solution.py:22
  396.4 0.1 reduce-scatter.11.cloned.1.call-update
  396.5 0.1 reduce-scatter.13.cloned.1.call-start
  396.6 22.4 %fusion.48 = bf16[640,2048]{1,0:T(8,128)(2,1)} fusion(bf16[4096,2048]{1,0:T(8,128)(2,1)} %convolution_convert_fusion.1, bf16[4096,640]{0,1:T(8,128)(2,1)} %get-tuple-element.27, f32[4096]{0:T(1024)S(1)} %copy-done.13, f32[4096,2048]{1,0:T(8,128)} %get-tuple-element.29), kind=kOutput, calls=%fused_computation.70 | convolution fusion | flops 10796924928 | bytes 58212352 | tf_op jit(solution)/shard_map/transpose(jvp())/dot_general | solution.py:22
  419.0 0.1 reduce-scatter.13.cloned.1.call-update
  419.0 0.1 reduce-scatter.7.cloned.1.call-start
  419.1 35.4 %fusion.51 = bf16[640,2048]{1,0:T(8,128)(2,1)} fusion(f32[4096,2048]{1,0:T(8,128)} %fusion.40, f32[4096,2048]{1,0:T(8,128)} %get-tuple-element.25, bf16[4096,2048]{1,0:T(8,128)(2,1)} %convolution_convert_fusion, bf16[1,4096,640]{1,2,0:T(8,128)(2,1)} %copy.20, f32[4096]{0:T(1024)S(1)} %copy-done.17), kind=kOutput, calls=%fused_computation.72 | convolution fusion | flops 10838867968 | bytes 91766784 | tf_op jit(solution)/shard_map/transpose(jvp())/dot_general | solution.py:21
  454.5 0.1 reduce-scatter.7.cloned.1.call-update
  454.5 0.1 reduce-scatter.9.cloned.1.call-start
  454.6 17.1 %fusion.42 = bf16[640,2048]{1,0:T(8,128)(2,1)} fusion(bf16[4096,2048]{1,0:T(8,128)(2,1)} %get-tuple-element.28, bf16[4096,640]{0,1:T(8,128)(2,1)} %get-tuple-element.27, f32[4096]{0:T(1024)S(1)} %copy-done.13), kind=kOutput, calls=%fused_computation.68 | convolution fusion | flops 10745282560 | bytes 24657920 | tf_op jit(solution)/shard_map/transpose(jvp())/dot_general | solution.py:21
  471.7 0.1 reduce-scatter.9.cloned.1.call-update
  471.8 2.6 fusion.70
  474.5 2.6 fusion.69
  477.0 14.7 %reduce-scatter.7.cloned.1.call-done = bf16[160,2048]{1,0:T(8,128)(2,1)} async-done(((bf16[640,2048]{1,0:T(8,128)(2,1)}), bf16[160,2048]{1,0:T(8,128)(2,1)}) %reduce-scatter.7.cloned.1.call-update) | async-done | bytes 655376 | tf_op jit(solution)/shard_map/reduce_scatter | solution.py:53
  491.7 32.4 %reduce-scatter.9.cloned.1.call-done = bf16[160,2048]{1,0:T(8,128)(2,1)} async-done(((bf16[640,2048]{1,0:T(8,128)(2,1)}), bf16[160,2048]{1,0:T(8,128)(2,1)}) %reduce-scatter.9.cloned.1.call-update) | async-done | bytes 655376 | tf_op jit(solution)/shard_map/reduce_scatter | solution.py:53
  524.1 2.7 fusion.68
  528.7 9.4 %psum.7 = f32[]{:T(128)} all-reduce(f32[]{:T(128)S(6)} %add.99), channel_id=1, replica_groups=mesh['rep'=4,'dp'=4] {'dp'}, use_global_device_ids=true, to_apply=%region_12.13 | all-reduce | flops 1 | bytes 8 | tf_op jit(solution)/shard_map/psum | solution.py:55
  538.9 6.1 %fusion.76 = (bf16[2,512,640]{2,1,0:T(8,128)(2,1)}, f32[2,512,640]{2,1,0:T(8,128)}, f32[2,512,640]{2,1,0:T(8,128)}) fusion(bf16[2,512,640]{2,1,0:T(8,128)(2,1)S(1)} %copy-done.1, f32[]{:T(128)S(6)} %min_shard_map.3, bf16[1,512,640]{2,1,0:T(8,128)(2,1)} %bitcast.71, bf16[1,512,640]{2,1,0:T(8,128)(2,1)} %bitcast.69, f32[2,512,640]{2,1,0:T(8,128)} %param.21, ...), kind=kLoop, calls=%fused_computation.91 | loop fusion | flops 13107200 | bytes 14417924 | tf_op jit(solution)/shard_map/convert_element_type | solution.py:30
  545.1 1.3 copy-done.5
  546.4 0.7 copy-done.6
  547.2 0.7 copy-done.7
  547.9 0.1 copy-done.8
  548.0 0.2 copy-done.9
  548.2 6.3 %fusion.67 = (bf16[2,160,2048]{2,1,0:T(8,128)(2,1)}, f32[2,160,2048]{2,1,0:T(8,128)}, f32[2,160,2048]{2,1,0:T(8,128)}, bf16[2,160,2048]{2,1,0:T(8,128)(2,1)}, f3...) fusion(bf16[2,160,2048]{2,1,0:T(8,128)(2,1)S(1)} %copy-done.2, f32[]{:T(128)S(6)} %min_shard_map.3, ...), kind=kLoop, calls=%fused_computation.82 | loop fusion | flops 26214400 | bytes 28835844 | tf_op jit(solution)/shard_map/convert_element_type | solution.py:30
  (43 shorter events, 0.2 us)
Async XLA Ops:
  7.2 5.4 copy-start
  7.2 36.6 %all-gather.13.cloned.1.call-start = ((), (), s32[]{:S(2)}) async-start(), calls=%async_computation.12 | async-start | bytes 3276800 | tf_op jit(solution)/shard_map/all_gather | solution.py:40
  9.9 67.0 %all-gather.15.cloned.1.call-start = ((), (), s32[]{:S(2)}) async-start(), calls=%async_computation.13 | async-start | bytes 3276800 | tf_op jit(solution)/shard_map/all_gather | solution.py:40
  12.5 98.4 %all-gather.17.cloned.1.call-start = ((), (), s32[]{:S(2)}) async-start(), calls=%async_computation.14 | async-start | bytes 3276800 | tf_op jit(solution)/shard_map/all_gather | solution.py:40
  13.8 129.1 %all-gather.21.cloned.1.call-start = ((), (), s32[]{:S(2)}) async-start(), calls=%async_computation.16 | async-start | bytes 3276800 | tf_op jit(solution)/shard_map/all_gather | solution.py:40
  14.5 161.4 %all-gather.23.cloned.1.call-start = ((), (), s32[]{:S(2)}) async-start(), calls=%async_computation.17 | async-start | bytes 3276800 | tf_op jit(solution)/shard_map/all_gather | solution.py:40
  15.1 193.7 %all-gather.19.cloned.1.call-start = ((), (), s32[]{:S(2)}) async-start(), calls=%async_computation.15 | async-start | bytes 3276800 | tf_op jit(solution)/shard_map/all_gather | solution.py:40
  15.8 456.0 %reduce-scatter.15.cloned.1.call-start = ((), (), s32[]{:S(2)}) async-start(), calls=%async_computation.10 | async-start | bytes 3276800 | tf_op jit(solution)/shard_map/reduce_scatter | solution.py:53
  27.4 49.5 %copy-start.16 = (f32[4096]{0:T(1024)}, f32[4096]{0:T(1024)S(1)}, u32[]{:S(2)}) copy-start(f32[4096]{0:T(1024)S(1)} %add_rsqrt_fusion) | copy-start | bytes 49156
  129.6 33.2 %copy-start.14 = (f32[4096]{0:T(1024)}, f32[4096]{0:T(1024)S(1)}, u32[]{:S(2)}) copy-start(f32[4096]{0:T(1024)S(1)} %get-tuple-element.26) | copy-start | bytes 49156
  129.6 166.6 %copy-start.12 = (f32[4096]{0:T(1024)}, f32[4096]{0:T(1024)S(1)}, u32[]{:S(2)}) copy-start(f32[4096]{0:T(1024)S(1)} %fusion.89) | copy-start | bytes 49156
  253.6 17.1 %copy-start.19 = (bf16[1,640,2048]{2,1,0:T(8,128)(2,1)S(1)}, bf16[1,640,2048]{2,1,0:T(8,128)(2,1)}, u32[]{:S(2)}) copy-start(bf16[1,640,2048]{2,1,0:T(8,128)(2,1)} %all-gather.23.cloned.1.call-done) | copy-start | bytes 7864324
  270.7 25.6 %copy-start.15 = (f32[4096]{0:T(1024)S(1)}, f32[4096]{0:T(1024)}, u32[]{:S(2)}) copy-start(f32[4096]{0:T(1024)} %copy-done.14) | copy-start | bytes 49156
  327.8 27.4 %copy-start.18 = (bf16[1,2048,640]{2,1,0:T(8,128)(2,1)S(1)}, bf16[1,2048,640]{2,1,0:T(8,128)(2,1)}, u32[]{:S(2)}) copy-start(bf16[1,2048,640]{2,1,0:T(8,128)(2,1)} %all-gather.17.cloned.1.call-done) | copy-start | bytes 7864324
  327.8 144.0 %reduce-scatter.17.cloned.1.call-start = ((), (), s32[]{:S(2)}) async-start(), calls=%async_computation.11 | async-start | bytes 3276800 | tf_op jit(solution)/shard_map/reduce_scatter | solution.py:53
  355.1 18.9 %copy-start.17 = (f32[4096]{0:T(1024)S(1)}, f32[4096]{0:T(1024)}, u32[]{:S(2)}) copy-start(f32[4096]{0:T(1024)} %copy-done.16) | copy-start | bytes 49156
  355.1 119.3 %reduce-scatter.11.cloned.1.call-start = ((), (), s32[]{:S(2)}) async-start(), calls=%async_computation.8 | async-start | bytes 3276800 | tf_op jit(solution)/shard_map/reduce_scatter | solution.py:53
  374.0 22.5 %copy-start.13 = (f32[4096]{0:T(1024)S(1)}, f32[4096]{0:T(1024)}, u32[]{:S(2)}) copy-start(f32[4096]{0:T(1024)} %copy-done.12) | copy-start | bytes 49156
  396.5 78.0 %reduce-scatter.13.cloned.1.call-start = ((), (), s32[]{:S(2)}) async-start(), calls=%async_computation.9 | async-start | bytes 3276800 | tf_op jit(solution)/shard_map/reduce_scatter | solution.py:53
  419.0 72.7 %reduce-scatter.7.cloned.1.call-start = ((), (), s32[]{:S(2)}) async-start(), calls=%async_computation.6 | async-start | bytes 3276800 | tf_op jit(solution)/shard_map/reduce_scatter | solution.py:53
  454.5 69.5 %reduce-scatter.9.cloned.1.call-start = ((), (), s32[]{:S(2)}) async-start(), calls=%async_computation.7 | async-start | bytes 3276800 | tf_op jit(solution)/shard_map/reduce_scatter | solution.py:53
  471.7 67.1 %copy-start.1 = (bf16[2,512,640]{2,1,0:T(8,128)(2,1)S(1)}, bf16[2,512,640]{2,1,0:T(8,128)(2,1)}, u32[]{:S(2)}) copy-start(bf16[2,512,640]{2,1,0:T(8,128)(2,1)} %param.15) | copy-start | bytes 3932164
  524.1 21.0 %copy-start.10 = (bf16[160,2048]{1,0:T(8,128)(2,1)S(1)}, bf16[160,2048]{1,0:T(8,128)(2,1)}, u32[]{:S(2)}) copy-start(bf16[160,2048]{1,0:T(8,128)(2,1)} %reduce-scatter.7.cloned.1.call-done) | copy-start | bytes 1966084
  524.1 21.0 %copy-start.11 = (bf16[160,2048]{1,0:T(8,128)(2,1)S(1)}, bf16[160,2048]{1,0:T(8,128)(2,1)}, u32[]{:S(2)}) copy-start(bf16[160,2048]{1,0:T(8,128)(2,1)} %reduce-scatter.9.cloned.1.call-done) | copy-start | bytes 1966084
  538.8 6.2 %copy-start.2 = (bf16[2,160,2048]{2,1,0:T(8,128)(2,1)S(1)}, bf16[2,160,2048]{2,1,0:T(8,128)(2,1)}, u32[]{:S(2)}) copy-start(bf16[2,160,2048]{2,1,0:T(8,128)(2,1)} %param.13) | copy-start | bytes 3932164
  538.8 6.2 %copy-start.3 = (bf16[2,160,2048]{2,1,0:T(8,128)(2,1)S(1)}, bf16[2,160,2048]{2,1,0:T(8,128)(2,1)}, u32[]{:S(2)}) copy-start(bf16[2,160,2048]{2,1,0:T(8,128)(2,1)} %param.14) | copy-start | bytes 3932164
  538.9 6.2 %copy-start.4 = (f32[2,160,2048]{2,1,0:T(8,128)S(1)}, f32[2,160,2048]{2,1,0:T(8,128)}, u32[]{:S(2)}) copy-start(f32[2,160,2048]{2,1,0:T(8,128)} %param.19) | copy-start | bytes 7864324
  538.9 7.6 %copy-start.5 = (f32[2,160,2048]{2,1,0:T(8,128)S(1)}, f32[2,160,2048]{2,1,0:T(8,128)}, u32[]{:S(2)}) copy-start(f32[2,160,2048]{2,1,0:T(8,128)} %param.16) | copy-start | bytes 7864324
  538.9 8.3 %copy-start.6 = (f32[2,160,2048]{2,1,0:T(8,128)S(1)}, f32[2,160,2048]{2,1,0:T(8,128)}, u32[]{:S(2)}) copy-start(f32[2,160,2048]{2,1,0:T(8,128)} %param.20) | copy-start | bytes 7864324
  538.9 9.0 %copy-start.7 = (f32[2,160,2048]{2,1,0:T(8,128)S(1)}, f32[2,160,2048]{2,1,0:T(8,128)}, u32[]{:S(2)}) copy-start(f32[2,160,2048]{2,1,0:T(8,128)} %param.17) | copy-start | bytes 7864324
  538.9 9.1 %copy-start.8 = (bf16[160,2048]{1,0:T(8,128)(2,1)S(1)}, bf16[160,2048]{1,0:T(8,128)(2,1)}, u32[]{:S(2)}) copy-start(bf16[160,2048]{1,0:T(8,128)(2,1)} %reduce-scatter.11.cloned.1.call-done) | copy-start | bytes 1966084
  538.9 9.3 %copy-start.9 = (bf16[160,2048]{1,0:T(8,128)(2,1)S(1)}, bf16[160,2048]{1,0:T(8,128)(2,1)}, u32[]{:S(2)}) copy-start(bf16[160,2048]{1,0:T(8,128)(2,1)} %reduce-scatter.13.cloned.1.call-done) | copy-start | bytes 1966084
Sparse Core Ops, SparseCore 0:
  10.2 33.5 all-gather.12
  45.9 30.9 all-gather.14
  79.0 30.9 all-gather.16
  111.9 30.9 all-gather.20
  144.9 30.9 all-gather.22
  177.8 30.9 all-gather.18
  327.9 30.1 reduce-scatter.14
  361.0 29.6 reduce-scatter.16
  396.6 30.1 reduce-scatter.10
  429.5 29.6 reduce-scatter.12
  462.0 29.6 reduce-scatter.6
  494.4 29.6 reduce-scatter.8
where the time goes:
time: 569 us; the launch traced here: 562 us
  matrix products  366 us (64%)
  waiting for transfers between devices  107 us (19%)
  other arithmetic  35.8 us (6%)
  local copies, waits for them, and re-layouts  25.3 us (4%)
  between operations  17.6 us (3%)
  blocking collectives  9.43 us (2%)
    dot_general x5, matrix products, layer(): gate = jnp.dot(a, w['w_gate'], preferred_element_type=jnp.float32)  136 us
    dot_general x5, matrix products, layer(): up = jnp.dot(a, w['w_up'], preferred_element_type=jnp.float32)  126 us
    dot_general x5, matrix products, matmul(): jnp.dot(a, w, preferred_element_type=jnp.float32).astype(jnp.bfloat16)  104 us
    all_gather x6, waiting for transfers between devices, fetched(): lax.all_gather(w[number], 'dp', axis=0, tiled=True)  57.3 us
    reduce_scatter x6, waiting for transfers between devices, step(): lax.psum_scatter(by_w[name], 'dp', scatter_dimension=0, tiled=True)  47.1 us
    unnamed x42, local copies, waits for them, and re-layouts  19.1 us
    convert_element_type x2, other arithmetic, adamw(): return ((w - 0.02 * step).astype(jnp.bfloat16), m, v)  12.4 us
    add_any x1, other arithmetic, normed(): wide = h.astype(jnp.float32)  11.9 us
  transfers between devices with their start and end apart: 12, of which 7 were waited for; matrix products, arithmetic and copies ran while one was open for 51% of the time, Pallas kernels for 0%

commit v1 on v0

v1 whole, which is shorter than its diff:
```python
import dataclasses
import functools

import jax
import jax.numpy as jnp
from jax import lax
from jax.experimental import pallas as pl
from jax.experimental.pallas import tpu as pltpu
from jax.sharding import PartitionSpec as P

BF, F32 = jnp.bfloat16, jnp.float32
LANES = 128
TILE = 512
VMEM_LIMIT = 67043328
NT = (((1,), (1,)), ((), ()))
NN = (((1,), (0,)), ((), ()))


@dataclasses.dataclass(frozen=True)
class Dims:
    layers: int
    tokens: int
    d: int
    ff: int
    n: int

    @property
    def own_ff(self):
        return self.ff // self.n

    @property
    def rows(self):
        return self.d // self.n

    @property
    def chunk(self):
        return self.n * LANES

    @property
    def chunks(self):
        return self.own_ff // LANES

    @property
    def tiles(self):
        return self.tokens // TILE

    @property
    def packed(self):
        return self.rows + self.d // 2 // self.n


def dot(a, b, dims=NN):
    return lax.dot_general(a, b, dims, preferred_element_type=F32)


def sliced(i, size):
    return pl.ds(pl.multiple_of(i * size, size), size)


def ring(n):
    me = lax.axis_index("dp")
    return me, lax.rem(me + 1, n), lax.rem(me + n - 1, n)


def partner():
    rep = lax.axis_index("rep")
    core = lax.rem(rep, 2)
    return core, rep + 1 - 2 * core


def greet(*others):
    barrier = pltpu.get_barrier_semaphore()
    for other in others:
        pl.semaphore_signal(barrier, inc=1, device_id=other, device_id_type=pl.DeviceIdType.MESH)
    pl.semaphore_wait(barrier, len(others))


def remote(src, dst, send, recv, device):
    return pltpu.make_async_remote_copy(src_ref=src, dst_ref=dst, send_sem=send, recv_sem=recv, device_id=device, device_id_type=pl.DeviceIdType.MESH)


class Gather:
    COPIES = 14

    def __init__(self, dm, w, sends, recvs):
        self.dm, self.w, self.sends, self.recvs = dm, w, sends, recvs
        self.me, self.right, self.left = ring(dm.n)
        self.far = lax.rem(self.me + 2, dm.n)
        self.core, self.other = partner()

    def _both(self, unit, source):
        half = self.dm.rows // 2
        at = pl.multiple_of(source * self.dm.rows + self.core * half, half)
        return self.w.at[unit, 0:2, pl.ds(at, half), :]

    def _one(self, unit, which, source):
        half = self.dm.rows // 2
        at = pl.multiple_of(source * self.dm.rows + self.core * half, half)
        return self.w.at[unit, which, pl.ds(at, half), :]

    def _down(self, unit, source, quarter=None):
        half = self.dm.d // 2
        columns = pl.ds(pl.multiple_of(source * LANES, LANES), LANES)
        if quarter is None:
            return self.w.at[unit, 2, pl.ds(pl.multiple_of(self.core * half, half), half), columns]
        return self.w.at[unit, 2, pl.ds(pl.multiple_of(self.core * half + quarter * (half // 2), half // 2), half // 2), columns]

    def _copy(self, unit, index, ref, device):
        return remote(ref, ref, self.sends.at[unit, index], self.recvs.at[unit, index], device)

    def own(self, unit):
        out = []
        for to, device in enumerate(({"dp": self.right}, {"dp": self.left})):
            out.append(self._copy(unit, 2 * to, self._both(unit, self.me), device))
            out.append(self._copy(unit, 2 * to + 1, self._down(unit, self.me), device))
        return out

    def relayed(self, unit):
        return [
            self._copy(unit, 4, self._one(unit, 0, self.left), {"dp": self.right}),
            self._copy(unit, 5, self._down(unit, self.left, 0), {"dp": self.right}),
            self._copy(unit, 6, self._one(unit, 1, self.right), {"dp": self.left}),
            self._copy(unit, 7, self._down(unit, self.right, 1), {"dp": self.left}),
        ]

    def shared(self, unit, sources):
        out = []
        for s in sources:
            source = (self.left, self.right, self.far)[s]
            out.append(self._copy(unit, 8 + 2 * s, self._both(unit, source), {"rep": self.other}))
            out.append(self._copy(unit, 9 + 2 * s, self._down(unit, source), {"rep": self.other}))
        return out

    def _arrivals(self, unit, index, ref):
        return remote(ref, ref, self.sends.at[unit, index], self.recvs.at[unit, index], {"dp": self.right})

    def step1(self, unit):
        for copy in self.own(unit):
            copy.start()

    def step2(self, unit):
        for to, source in enumerate((self.left, self.right)):
            self._arrivals(unit, 2 * to, self._both(unit, source)).wait_recv()
            self._arrivals(unit, 2 * to + 1, self._down(unit, source)).wait_recv()
        for copy in self.relayed(unit) + self.shared(unit, (0, 1)):
            copy.start()

    def step3(self, unit):
        self._arrivals(unit, 4, self._one(unit, 0, self.far)).wait_recv()
        self._arrivals(unit, 5, self._down(unit, self.far, 0)).wait_recv()
        self._arrivals(unit, 6, self._one(unit, 1, self.far)).wait_recv()
        self._arrivals(unit, 7, self._down(unit, self.far, 1)).wait_recv()
        for copy in self.shared(unit, (2,)):
            copy.start()

    def _theirs(self, unit, s):
        dm, other = self.dm, 1 - self.core
        source = (self.left, self.right, self.far)[s]
        half = dm.rows // 2
        at = pl.multiple_of(source * dm.rows + other * half, half)
        columns = pl.ds(pl.multiple_of(source * LANES, LANES), LANES)
        rows = pl.ds(pl.multiple_of(other * (dm.d // 2), dm.d // 2), dm.d // 2)
        return self.w.at[unit, 0:2, pl.ds(at, half), :], self.w.at[unit, 2, rows, columns]

    def done(self, unit):
        for s in range(3):
            both, down = self._theirs(unit, s)
            self._arrivals(unit, 8 + 2 * s, both).wait_recv()
            self._arrivals(unit, 9 + 2 * s, down).wait_recv()

    def drain(self, unit):
        for copy in self.own(unit) + self.relayed(unit) + self.shared(unit, (0, 1, 2)):
            copy.wait_send()


def fetch_own(dm, layer, chunk, unit, me, w, sources, sem):
    for which in range(2):
        for q in range(dm.n):
            pltpu.make_async_copy(
                sources[which].at[layer, :, pl.ds(q * dm.own_ff + chunk * LANES, LANES)],
                w.at[unit, which, sliced(me, dm.rows), pl.ds(q * LANES, LANES)],
                sem,
            ).start()


def await_own(dm, unit, me, w, sem):
    ref = w.at[unit, 0:2, sliced(me, dm.rows), :]
    pltpu.make_async_copy(ref, ref, sem).wait()


def scale_of(wide, axis, count):
    return lax.rsqrt(jnp.sum(wide * wide, axis, keepdims=True) / count + 1e-6)


def forward_kernel(
    dm, extra, x, dy, w_gate, w_up, w_down,
    gates, ups, a1, a1t, h1t, a0t, dyt, wd0, w1,
    abuf, xt, at, ht, w, gst, ust, natural, dyb, dytb,
    own_sem, nat_sem, x_sem, dy_sem, dyt_sem, st_sem, at_sem, out_sem, w_sem, sends, recvs,
):
    tiles, units = dm.tiles, dm.chunks + extra
    gather = Gather(dm, w, sends, recvs)
    me = gather.me
    place = lambda u: (u // dm.chunks, u % dm.chunks)
    for u in range(units):
        fetch_own(dm, *place(u), u, me, w, (w_gate, w_up), own_sem.at[u])
    for layer in range(2):
        pltpu.make_async_copy(w_down.at[layer], natural.at[layer], nat_sem.at[layer]).start()
    for t in range(tiles):
        pltpu.make_async_copy(x.at[pl.ds(t * TILE, TILE), :], abuf.at[pl.ds(t * TILE, TILE), :], x_sem.at[t]).start()
    for t in range(2):
        pltpu.make_async_copy(dy.at[pl.ds(t * TILE, TILE), :], dyb.at[t], dy_sem.at[t]).start()
    greet({"dp": gather.right}, {"dp": gather.left}, {"rep": gather.other})
    for layer in range(2):
        pltpu.make_async_copy(w_down.at[layer], natural.at[layer], nat_sem.at[layer]).wait()
    columns = pl.ds(pl.multiple_of(me * LANES, LANES), LANES)
    for u in range(units):
        layer, chunk = place(u)
        w[u, 2, :, columns] = natural[layer, pl.ds(chunk * LANES, LANES), :].T
    await_own(dm, 0, me, w, own_sem.at[0])
    gather.step1(0)

    @pl.loop(0, tiles)
    def _(t):
        at_t = sliced(t, TILE)
        pltpu.make_async_copy(x.at[at_t, :], abuf.at[at_t, :], x_sem.at[t]).wait()
        tile = abuf[at_t, :]
        wide = tile.astype(F32)
        a = (wide * scale_of(wide, -1, dm.d)).astype(BF)
        xt[:, at_t] = tile.T
        at[:, at_t] = a.T
        abuf[at_t, :] = a

    pltpu.make_async_copy(at, a0t, at_sem.at[0]).start()
    await_own(dm, 1, me, w, own_sem.at[1])
    gather.step2(0)
    gather.step1(1)

    @pl.loop(0, tiles)
    def _(t):
        slot = lax.rem(t, 2)

        @pl.when(t >= 2)
        def _():
            pltpu.make_async_copy(dytb.at[slot], dyt.at[:, sliced(t - 2, TILE)], dyt_sem.at[slot]).wait()

        pltpu.make_async_copy(dy.at[sliced(t, TILE), :], dyb.at[slot], dy_sem.at[slot]).wait()
        dytb[slot] = dyb[slot].T
        pltpu.make_async_copy(dytb.at[slot], dyt.at[:, sliced(t, TILE)], dyt_sem.at[slot]).start()

        @pl.when(t + 2 < tiles)
        def _():
            pltpu.make_async_copy(dy.at[sliced(t + 2, TILE), :], dyb.at[slot], dy_sem.at[slot]).start()

    for t in range(tiles - 2, tiles):
        pltpu.make_async_copy(dytb.at[t % 2], dyt.at[:, pl.ds(t * TILE, TILE)], dyt_sem.at[t % 2]).wait()
    gather.step3(0)

    def stored(i, which):
        slot, chunk, at_t = lax.rem(i, 2), i // tiles, sliced(lax.rem(i, tiles), TILE)
        return pltpu.make_async_copy((gst, ust)[which].at[slot], (gates, ups)[which].at[chunk, at_t, :], st_sem.at[which, slot])

    def results(t):
        at_t = sliced(t, TILE)
        return (
            pltpu.make_async_copy(abuf.at[at_t, :], a1.at[at_t, :], out_sem.at[0, t]),
            pltpu.make_async_copy(at.at[:, at_t], a1t.at[:, at_t], out_sem.at[1, t]),
            pltpu.make_async_copy(xt.at[:, at_t], h1t.at[:, at_t], out_sem.at[2, t]),
        )

    def tile_step(i, last):
        c, t = i // tiles, lax.rem(i, tiles)
        slot, at_t = lax.rem(i, 2), sliced(t, TILE)

        @pl.when(t == 0)
        def _():
            gather.done(c)
            if last:
                pltpu.make_async_copy(w.at[0 : dm.chunks, 2], wd0, w_sem.at[0]).start()

        @pl.when(jnp.logical_and(t == 1, c + 1 < units))
        def _():
            gather.step2(c + 1)

        @pl.when(jnp.logical_and(t == 1, c + 2 < units))
        def _():
            await_own(dm, c + 2, me, w, own_sem.at[c + 2])
            gather.step1(c + 2)

        @pl.when(jnp.logical_and(t == 5, c + 1 < units))
        def _():
            gather.step3(c + 1)

        @pl.when(i >= 2)
        def _():
            stored(i - 2, 0).wait()
            stored(i - 2, 1).wait()

        a = abuf[at_t, :]
        gate = dot(a, w[c, 0])
        up = dot(a, w[c, 1])
        gst[slot] = gate
        ust[slot] = up
        act = (gate * jax.nn.sigmoid(gate) * up).astype(BF)
        total = jnp.where(c == 0, 0.0, ht[:, at_t]) + dot(w[c, 2], act, NT)
        if last:
            h = xt[:, at_t] + total.astype(BF)
            wide = h.astype(F32)
            a = (wide * scale_of(wide, 0, dm.d)).astype(BF)
            xt[:, at_t] = h
            at[:, at_t] = a
            abuf[at_t, :] = a.T
        else:
            ht[:, at_t] = total
        stored(i, 0).start()
        stored(i, 1).start()
        if last:
            for copy in results(t):
                copy.start()

    steps = dm.chunks * tiles

    @pl.loop(0, steps - tiles)
    def _(i):
        tile_step(i, False)

    pltpu.make_async_copy(at, a0t, at_sem.at[0]).wait()

    @pl.loop(steps - tiles, steps)
    def _(i):
        tile_step(i, True)

    for u in range(dm.chunks, units):
        gather.done(u)
    pltpu.make_async_copy(w.at[dm.chunks : units], w1, w_sem.at[1]).start()
    for i in range(steps - 2, steps):
        stored(i, 0).wait()
        stored(i, 1).wait()
    for t in range(tiles):
        for copy in results(t):
            copy.wait()
    pltpu.make_async_copy(w.at[0 : dm.chunks, 2], wd0, w_sem.at[0]).wait()
    pltpu.make_async_copy(w.at[dm.chunks : units], w1, w_sem.at[1]).wait()
    for u in range(units):
        gather.drain(u)


class Scatter:
    def __init__(self, dm, acc, send, recv, sends, recvs):
        self.dm, self.acc, self.send, self.recv, self.sends, self.recvs = dm, acc, send, recv, sends, recvs
        self.me, self.right, self.left = ring(dm.n)
        self.far = lax.rem(self.me + 2, dm.n)

    def _copy(self, c, kind):
        device = {"dp": self.right if kind % 2 == 0 else self.left}
        slot = lax.rem(c, 2)
        return remote(self.send.at[kind], self.recv.at[slot, kind], self.sends.at[kind], self.recvs.at[slot, kind], device)

    def _parts(self, c, owner, half):
        dm, slot = self.dm, lax.rem(c, 2)
        wide = self.acc[slot, half, sliced(owner, dm.rows), :]
        columns = pl.ds(pl.multiple_of(owner * LANES, LANES), LANES)
        size = dm.d // 2 // dm.n
        pieces = [self.acc[slot, 2, pl.ds(half * (dm.d // 2) + i * size, size), columns] for i in range(dm.n)]
        return wide, pieces

    def _places(self):
        dm = self.dm
        yield (slice(0, dm.rows), slice(None))
        for i in range(dm.n):
            yield (slice(dm.rows, dm.packed), slice(i * LANES, (i + 1) * LANES))

    def _put(self, c, kind, owner, half, add=None):
        wide, pieces = self._parts(c, owner, half)
        for term, (rows, columns) in zip([wide] + pieces, self._places(), strict=True):
            if add is not None:
                term = term + self.recv[lax.rem(c, 2), add, rows, columns].astype(F32)
            self.send[kind, rows, columns] = term.astype(BF)
        self._copy(c, kind).start()

    def step1(self, c):
        self._put(c, 0, self.far, 0)
        self._put(c, 1, self.far, 1)
        self._put(c, 2, self.right, 1)
        self._put(c, 3, self.left, 0)

    def step2(self, c):
        for kind, owner, half in ((0, self.right, 0), (1, self.left, 1)):
            self._copy(c, kind).wait_recv()
            self._put(c, kind + 4, owner, half, add=kind)
        for kind in (0, 1):
            self._copy(c, kind).wait_send()

    def step3(self, c, grads, squares):
        for kind in (2, 3, 4, 5):
            self._copy(c, kind).wait_recv()
        slot = lax.rem(c, 2)
        for half, kinds in ((0, (4, 3)), (1, (2, 5))):
            wide, pieces = self._parts(c, self.me, half)
            for term, (rows, columns) in zip([wide] + pieces, self._places(), strict=True):
                for kind in kinds:
                    term = term + self.recv[slot, kind, rows, columns].astype(F32)
                g = term.astype(BF)
                grads[c, half, rows, columns] = g
                g = g.astype(F32)
                g = jnp.sum((g * g).reshape(-1, 8, g.shape[-1]), 0)
                for j in range(0, g.shape[-1], LANES):
                    squares[...] += g[:, j : j + LANES]
        for kind in (2, 3, 4, 5):
            self._copy(c, kind).wait_send()


def elementwise(gate, up, by_act):
    by_act = by_act.astype(BF).astype(F32)
    s = jax.nn.sigmoid(gate)
    silu = gate * s
    act = (silu * up).astype(BF)
    by_up = (by_act * silu).astype(BF)
    by_gate = (by_act * up * (s * (1.0 + gate * (1.0 - s)))).astype(BF)
    return act, by_gate, by_up


def add_gradients(acc, slot, first, at, dyt, act, by_gate, by_up):
    for which, (left, right) in enumerate(((at, by_gate), (at, by_up), (dyt, act))):
        acc[slot, which] = jnp.where(first, 0.0, acc[slot, which]) + dot(left, right)


def backward1_kernel(
    dm, a1, a1t, dy, dyt, h1t, w_gate, w_up, w_down, w1,
    grads_out, squares_out, dh, dht, by_gates, by_ups,
    abuf, at, dyb, dytb, w, natural, acc, bg, bu, bg2, bu2, hb, dhb, dhtb, send, recv, grads, squares,
    own_sem, nat_sem, w_sem, in_sem, b_sem, b2_sem, h_sem, o_sem, g_sem, sends, recvs, rsends, rrecvs,
):
    tiles, units = dm.tiles, dm.chunks
    gather = Gather(dm, w, sends, recvs)
    scatter = Scatter(dm, acc, send, recv, rsends, rrecvs)
    me, layer = gather.me, 1
    loads = lambda t: (
        pltpu.make_async_copy(a1.at[sliced(t, TILE), :], abuf.at[sliced(t, TILE), :], in_sem.at[0, t]),
        pltpu.make_async_copy(dy.at[sliced(t, TILE), :], dyb.at[sliced(t, TILE), :], in_sem.at[1, t]),
        pltpu.make_async_copy(a1t.at[:, sliced(t, TILE)], at.at[:, sliced(t, TILE)], in_sem.at[2, t]),
        pltpu.make_async_copy(dyt.at[:, sliced(t, TILE)], dytb.at[:, sliced(t, TILE)], in_sem.at[3, t]),
    )
    pltpu.make_async_copy(w1.at[0], w.at[0], w_sem.at[0]).start()
    for copy in loads(0):
        copy.start()
    for u in range(1, units):
        fetch_own(dm, layer, u, u, me, w, (w_gate, w_up), own_sem.at[u])
    pltpu.make_async_copy(w_down.at[layer], natural, nat_sem.at[0]).start()
    for t in range(1, tiles):
        for copy in loads(t):
            copy.start()
    greet({"dp": gather.right}, {"dp": gather.left}, {"rep": gather.other})
    pltpu.make_async_copy(w_down.at[layer], natural, nat_sem.at[0]).wait()
    columns = pl.ds(pl.multiple_of(me * LANES, LANES), LANES)
    for u in range(1, units):
        w[u, 2, :, columns] = natural[pl.ds(u * LANES, LANES), :].T
    await_own(dm, 1, me, w, own_sem.at[1])
    gather.step1(1)
    squares[...] = jnp.zeros_like(squares)
    pltpu.make_async_copy(w1.at[0], w.at[0], w_sem.at[0]).wait()

    def stored(i, which):
        slot, chunk, at_t = lax.rem(i, 2), i // tiles, sliced(lax.rem(i, tiles), TILE)
        return pltpu.make_async_copy((bg, bu)[which].at[slot], (by_gates, by_ups)[which].at[chunk, at_t, :], b_sem.at[which, slot])

    steps = dm.chunks * tiles

    @pl.loop(0, steps)
    def _(i):
        c, t = i // tiles, lax.rem(i, tiles)
        slot, at_t = lax.rem(i, 2), sliced(t, TILE)

        @pl.when(c == 0)
        def _():
            for copy in loads(t):
                copy.wait()

        @pl.when(jnp.logical_and(t == 0, c >= 1))
        def _():
            gather.done(c)
            scatter.step1(c - 1)

        @pl.when(i == 2)
        def _():
            gather.step2(1)
            await_own(dm, 2, me, w, own_sem.at[2])
            gather.step1(2)

        @pl.when(i == 4)
        def _():
            gather.step3(1)

        @pl.when(i == 5)
        def _():
            gather.step2(2)
            await_own(dm, 3, me, w, own_sem.at[3])
            gather.step1(3)

        @pl.when(i == 7)
        def _():
            gather.step3(2)

        @pl.when(i == tiles + 1)
        def _():
            gather.step2(3)

        @pl.when(i == tiles + 3)
        def _():
            gather.step3(3)

        @pl.when(jnp.logical_and(t == 5, c >= 1))
        def _():
            scatter.step2(c - 1)

        @pl.when(jnp.logical_and(t == 7, c >= 1))
        def _():
            scatter.step3(c - 1, grads, squares)

        @pl.when(i >= 2)
        def _():
            stored(i - 2, 0).wait()
            stored(i - 2, 1).wait()

        a = abuf[at_t, :]
        act, by_gate, by_up = elementwise(dot(a, w[c, 0]), dot(a, w[c, 1]), dot(dyb[at_t, :], w[c, 2]))
        bg[slot] = by_gate
        bu[slot] = by_up
        add_gradients(acc, lax.rem(c, 2), t == 0, at[:, at_t], dytb[:, at_t], act, by_gate, by_up)
        stored(i, 0).start()
        stored(i, 1).start()

    last = dm.chunks - 1
    scatter.step1(last)
    for i in range(steps - 2, steps):
        stored(i, 0).wait()
        stored(i, 1).wait()

    def inputs(t):
        slot, at_t = lax.rem(t, 2), sliced(t, TILE)
        return (
            pltpu.make_async_copy(by_gates.at[:, at_t, :], bg2.at[slot], b2_sem.at[0, slot]),
            pltpu.make_async_copy(by_ups.at[:, at_t, :], bu2.at[slot], b2_sem.at[1, slot]),
            pltpu.make_async_copy(h1t.at[:, at_t], hb.at[slot], h_sem.at[slot]),
        )

    def results(t):
        slot, at_t = lax.rem(t, 2), sliced(t, TILE)
        return (
            pltpu.make_async_copy(dhb.at[slot], dh.at[at_t, :], o_sem.at[0, slot]),
            pltpu.make_async_copy(dhtb.at[slot], dht.at[:, at_t], o_sem.at[1, slot]),
        )

    for copy in inputs(0):
        copy.start()

    @pl.loop(0, tiles)
    def _(t):
        slot, at_t = lax.rem(t, 2), sliced(t, TILE)

        @pl.when(t + 1 < tiles)
        def _():
            for copy in inputs(t + 1):
                copy.start()

        @pl.when(t == 3)
        def _():
            scatter.step2(last)

        @pl.when(t == 6)
        def _():
            scatter.step3(last, grads, squares)

        for copy in inputs(t):
            copy.wait()

        @pl.when(t >= 2)
        def _():
            for copy in results(t - 2):
                copy.wait()

        by_a = jnp.zeros((dm.d, TILE), F32)
        for c in range(dm.chunks):
            by_a = by_a + dot(w[c, 0], bg2[slot, c], NT) + dot(w[c, 1], bu2[slot, c], NT)
        by_a = by_a.astype(BF).astype(F32)
        h = hb[slot].astype(F32)
        square = jnp.sum(h * h, 0, keepdims=True) / dm.d + 1e-6
        scale = lax.rsqrt(square)
        along = jnp.sum(h * by_a, 0, keepdims=True) * (scale / square) / dm.d
        by_h = dytb[:, at_t] + (by_a * scale - h * along).astype(BF)
        dhtb[slot] = by_h
        dhb[slot] = by_h.T
        for copy in results(t):
            copy.start()

    for t in range(tiles - 2, tiles):
        for copy in results(t):
            copy.wait()
    for u in range(1, units):
        gather.drain(u)
    pltpu.make_async_copy(grads, grads_out, g_sem.at[0]).start()
    pltpu.make_async_copy(squares, squares_out, g_sem.at[1]).start()
    pltpu.make_async_copy(grads, grads_out, g_sem.at[0]).wait()
    pltpu.make_async_copy(squares, squares_out, g_sem.at[1]).wait()


def backward0_kernel(
    dm, dh, dht, a0t, gates, ups, wd0, grads1, squares1,
    grads_out, total_out,
    dhb, dhtb, at, wd, gb, ub, acc, send, recv, grads, squares, everyone,
    in_sem, w_sem, gu_sem, g_sem, rsends, rrecvs, ssends, srecvs,
):
    tiles = dm.tiles
    scatter = Scatter(dm, acc, send, recv, rsends, rrecvs)
    me = scatter.me
    loads = lambda t: (
        pltpu.make_async_copy(dh.at[sliced(t, TILE), :], dhb.at[sliced(t, TILE), :], in_sem.at[0, t]),
        pltpu.make_async_copy(dht.at[:, sliced(t, TILE)], dhtb.at[:, sliced(t, TILE)], in_sem.at[1, t]),
        pltpu.make_async_copy(a0t.at[:, sliced(t, TILE)], at.at[:, sliced(t, TILE)], in_sem.at[2, t]),
    )

    def inputs(i):
        slot, chunk, at_t = lax.rem(i, 2), i // tiles, sliced(lax.rem(i, tiles), TILE)
        return (
            pltpu.make_async_copy(gates.at[chunk, at_t, :], gb.at[slot], gu_sem.at[0, slot]),
            pltpu.make_async_copy(ups.at[chunk, at_t, :], ub.at[slot], gu_sem.at[1, slot]),
        )

    pltpu.make_async_copy(wd0, wd, w_sem.at[0]).start()
    for copy in (*loads(0), *inputs(0)):
        copy.start()
    for t in range(1, tiles):
        for copy in loads(t):
            copy.start()
    pltpu.make_async_copy(grads1, grads.at[1], g_sem.at[0]).start()
    pltpu.make_async_copy(squares1, squares, g_sem.at[1]).start()
    greet({"dp": scatter.right}, {"dp": scatter.left}, {"dp": scatter.far})
    pltpu.make_async_copy(squares1, squares, g_sem.at[1]).wait()
    pltpu.make_async_copy(wd0, wd, w_sem.at[0]).wait()
    steps = dm.chunks * tiles

    @pl.loop(0, steps)
    def _(i):
        c, t = i // tiles, lax.rem(i, tiles)
        slot, at_t = lax.rem(i, 2), sliced(t, TILE)

        @pl.when(c == 0)
        def _():
            for copy in loads(t):
                copy.wait()

        @pl.when(i + 1 < steps)
        def _():
            for copy in inputs(i + 1):
                copy.start()

        @pl.when(jnp.logical_and(t == 0, c >= 2))
        def _():
            scatter.step3(c - 2, grads.at[0], squares)

        @pl.when(jnp.logical_and(t == 0, c >= 1))
        def _():
            scatter.step1(c - 1)

        @pl.when(jnp.logical_and(t == 7, c >= 1))
        def _():
            scatter.step2(c - 1)

        for copy in inputs(i):
            copy.wait()
        act, by_gate, by_up = elementwise(gb[slot], ub[slot], dot(dhb[at_t, :], wd[c]))
        add_gradients(acc, lax.rem(c, 2), t == 0, at[:, at_t], dhtb[:, at_t], act, by_gate, by_up)

    last = dm.chunks - 1
    scatter.step3(last - 1, grads.at[0], squares)
    scatter.step1(last)
    scatter.step2(last)
    scatter.step3(last, grads.at[0], squares)
    pltpu.make_async_copy(grads1, grads.at[1], g_sem.at[0]).wait()
    pltpu.make_async_copy(grads, grads_out, g_sem.at[2]).start()

    copies = []
    for k in range(1, dm.n):
        to = lax.rem(me + k, dm.n)
        copies.append(remote(squares, everyone.at[me], ssends.at[k - 1], srecvs.at[k - 1], {"dp": to}))
    for copy in copies:
        copy.start()
    everyone[me] = squares[...]
    for copy in copies:
        copy.wait()
    total = everyone[0]
    for k in range(1, dm.n):
        total = total + everyone[k]
    total_out[...] = total
    pltpu.make_async_copy(grads, grads_out, g_sem.at[2]).wait()


def optimizer_kernel(dm, total, grads, *refs):
    ins, outs = refs[:9], refs[9:]
    count = dm.layers * 3 * dm.d * dm.ff
    factor = jnp.minimum(1.0, 0.5 * lax.rsqrt(jnp.sum(total[...]) / count + 1e-30))
    layer, q = pl.program_id(0), pl.program_id(1)
    size = dm.d // 2 // dm.n
    wide = [
        jnp.concatenate([grads[layer, c, half, 0 : dm.rows, pl.ds(pl.multiple_of(q * LANES, LANES), LANES)] for c in range(dm.chunks)], axis=1)
        for half in range(2)
    ]
    down = jnp.concatenate(
        [grads[layer, q, half, dm.rows : dm.packed, i * LANES : (i + 1) * LANES] for half in range(2) for i in range(dm.n)], axis=0
    ).T
    for which, g in enumerate((*wide, down)):
        w, m, v = (ins[which + 3 * j][0] for j in range(3))
        g = g.astype(F32) * factor
        w = w.astype(F32)
        m = 0.9 * m + 0.1 * g
        v = 0.95 * v + 0.05 * g * g
        step = m * lax.rsqrt(v + 1e-8) + 0.1 * w
        outs[which][0] = (w - 0.02 * step).astype(BF)
        outs[which + 3][0] = m
        outs[which + 6][0] = v


def step(mesh, x, dy, *arrays):
    weights, m, v = (arrays[i : i + 3] for i in (0, 3, 6))
    x, dy = x[0], dy[0]
    w_gate, w_up, w_down = weights
    n = mesh.shape["dp"]
    dm = Dims(w_gate.shape[0], x.shape[0], x.shape[1], w_gate.shape[2], n)
    tokens, d, chunk, chunks, tiles = dm.tokens, dm.d, dm.chunk, dm.chunks, dm.tiles
    hbm = pl.BlockSpec(memory_space=pltpu.HBM)
    vmem = pl.BlockSpec(memory_space=pltpu.VMEM)
    shape = jax.ShapeDtypeStruct
    dma = lambda *s: pltpu.SemaphoreType.DMA(s)
    params = lambda i: pltpu.CompilerParams(vmem_limit_bytes=VMEM_LIMIT, collective_id=i, has_side_effects=True)
    natural, turned = (tokens, d), (d, tokens)

    extra = 1
    units = chunks + extra
    gates, ups, a1, a1t, h1t, a0t, dyt, wd0, w1 = pl.pallas_call(
        functools.partial(forward_kernel, dm, extra),
        out_shape=[
            shape((chunks, tokens, chunk), F32), shape((chunks, tokens, chunk), F32), shape(natural, BF), shape(turned, BF), shape(turned, BF),
            shape(turned, BF), shape(turned, BF), shape((chunks, d, chunk), BF), shape((extra, 3, d, chunk), BF),
        ],
        in_specs=[hbm] * 5,
        out_specs=[hbm] * 9,
        scratch_shapes=[
            pltpu.VMEM(natural, BF), pltpu.VMEM(turned, BF), pltpu.VMEM(turned, BF), pltpu.VMEM(turned, F32),
            pltpu.VMEM((units, 3, d, chunk), BF), pltpu.VMEM((2, TILE, chunk), F32), pltpu.VMEM((2, TILE, chunk), F32),
            pltpu.VMEM((2, dm.own_ff, d), BF), pltpu.VMEM((2, TILE, d), BF), pltpu.VMEM((2, d, TILE), BF),
            dma(units), dma(2), dma(tiles), dma(2), dma(2), dma(2, 2), dma(1), dma(3, tiles), dma(2),
            dma(units, Gather.COPIES), dma(units, Gather.COPIES),
        ],
        compiler_params=params(0),
        name="forward",
    )(x, dy, w_gate, w_up, w_down)

    block = (dm.packed, chunk)
    grads1, squares1, dh, dht, _, _ = pl.pallas_call(
        functools.partial(backward1_kernel, dm),
        out_shape=[
            shape((chunks, 2, *block), BF), shape((8, LANES), F32), shape(natural, BF), shape(turned, BF),
            shape((chunks, tokens, chunk), BF), shape((chunks, tokens, chunk), BF),
        ],
        in_specs=[hbm] * 9,
        out_specs=[hbm] * 6,
        scratch_shapes=[
            pltpu.VMEM(natural, BF), pltpu.VMEM(turned, BF), pltpu.VMEM(natural, BF), pltpu.VMEM(turned, BF),
            pltpu.VMEM((chunks, 3, d, chunk), BF), pltpu.VMEM((dm.own_ff, d), BF), pltpu.VMEM((2, 3, d, chunk), F32),
            pltpu.VMEM((2, TILE, chunk), BF), pltpu.VMEM((2, TILE, chunk), BF),
            pltpu.VMEM((2, chunks, TILE, chunk), BF), pltpu.VMEM((2, chunks, TILE, chunk), BF), pltpu.VMEM((2, d, TILE), BF),
            pltpu.VMEM((2, TILE, d), BF), pltpu.VMEM((2, d, TILE), BF),
            pltpu.VMEM((6, *block), BF), pltpu.VMEM((2, 6, *block), BF), pltpu.VMEM((chunks, 2, *block), BF), pltpu.VMEM((8, LANES), F32),
            dma(chunks), dma(1), dma(1), dma(4, tiles), dma(2, 2), dma(2, 2), dma(2), dma(2, 2), dma(2),
            dma(chunks, Gather.COPIES), dma(chunks, Gather.COPIES), dma(6), dma(2, 6),
        ],
        compiler_params=params(1),
        name="backward1",
    )(a1, a1t, dy, dyt, h1t, w_gate, w_up, w_down, w1)

    grads, total = pl.pallas_call(
        functools.partial(backward0_kernel, dm),
        out_shape=[shape((2, chunks, 2, *block), BF), shape((8, LANES), F32)],
        in_specs=[hbm] * 8,
        out_specs=[hbm, vmem],
        scratch_shapes=[
            pltpu.VMEM(natural, BF), pltpu.VMEM(turned, BF), pltpu.VMEM(turned, BF), pltpu.VMEM((chunks, d, chunk), BF),
            pltpu.VMEM((2, TILE, chunk), F32), pltpu.VMEM((2, TILE, chunk), F32), pltpu.VMEM((2, 3, d, chunk), F32),
            pltpu.VMEM((6, *block), BF), pltpu.VMEM((2, 6, *block), BF), pltpu.VMEM((2, chunks, 2, *block), BF), pltpu.VMEM((8, LANES), F32),
            pltpu.VMEM((n, 8, LANES), F32),
            dma(3, tiles), dma(1), dma(2, 2), dma(3), dma(6), dma(2, 6), dma(n - 1), dma(n - 1),
        ],
        compiler_params=params(2),
        name="backward0",
    )(dh, dht, a0t, gates, ups, wd0, grads1, squares1)

    wide = pl.BlockSpec((1, dm.rows, chunks * LANES), lambda l, q: (l, 0, q))
    down = pl.BlockSpec((1, LANES, d), lambda l, q: (l, q, 0))
    whole = lambda s: pl.BlockSpec(s, lambda l, q: (0,) * len(s))
    return tuple(
        pl.pallas_call(
            functools.partial(optimizer_kernel, dm),
            out_shape=[shape(w.shape, BF) for w in weights] + [shape(w.shape, F32) for w in weights] * 2,
            grid=(dm.layers, dm.n),
            in_specs=[whole((8, LANES)), whole((2, chunks, 2, *block))] + [wide, wide, down] * 3,
            out_specs=[wide, wide, down] * 3,
            compiler_params=pltpu.CompilerParams(dimension_semantics=("arbitrary", "arbitrary")),
            name="optimizer",
        )(total, grads, *weights, *m, *v)
    )


def solution(mesh):
    states, cut = P(("rep", "dp"), None, None), P(None, "dp", None)
    return jax.shard_map(
        functools.partial(step, mesh),
        mesh=mesh,
        in_specs=(states, states) + (cut,) * 9,
        out_specs=(P("rep", "dp", None),) * 9,
        check_vma=False,
    )
```

time: 569 us -> 348 us (0.61); the launches traced: 562 us -> 348 us
  matrix products: 366 us -> 0 us
  Pallas kernels: 0 us -> 347 us
  waiting for transfers between devices: 107 us -> 0 us
  other arithmetic: 35.8 us -> 0 us
  local copies, waits for them, and re-layouts: 25.3 us -> 0 us
  between operations: 17.6 us -> 0.83 us
  blocking collectives: 9.43 us -> 0 us
    dot_general x15 -> x0, matrix products: 366 us -> none  [the longest x5 136 us: layer(): gate = jnp.dot(a, w['w_gate'], preferred_element_type=jnp.float32)]
    pallas_call x0 -> x4, Pallas kernels: none -> 347 us  [the longest x1 145 us: step(): pl.pallas_call(functools.partial(backward1_kernel, dm), out_shape=[shape(...]
    all_gather x6 -> x0, waiting for transfers between devices: 57.3 us -> none  [fetched(): lax.all_gather(w[number], 'dp', axis=0, tiled=True)]
    reduce_scatter x6 -> x0, waiting for transfers between devices: 47.1 us -> none  [step(): lax.psum_scatter(by_w[name], 'dp', scatter_dimension=0, tiled=True)]
    unnamed x42 -> x0, local copies, waits for them, and re-layouts: 19.1 us -> none
    convert_element_type x2 -> x0, other arithmetic: 12.4 us -> none  [adamw(): return ((w - 0.02 * step).astype(jnp.bfloat16), m, v)]
    add_any x1 -> x0, other arithmetic: 11.9 us -> none  [normed(): wide = h.astype(jnp.float32)]
    reduce_sum x4 -> x0, other arithmetic: 11.5 us -> none  [the longest x3 7.88 us: step(): squares = lax.psum(sum((jnp.sum(g * g) for g in gradients)), 'dp')]
  transfers between devices with their start and end apart: 12 -> 0, of which waited for: 7 -> 0; matrix products, arithmetic and copies ran while one was open for 51% -> 0% of each run, Pallas kernels for 0% -> 0%
where the time goes in v1:
time: 348 us
  Pallas kernels  347 us (100%)
    pallas_call x1, Pallas kernels, step(): pl.pallas_call(functools.partial(backward1_kernel, dm), out_shape=[shape(...  145 us
    pallas_call x1, Pallas kernels, step(): pl.pallas_call(functools.partial(backward0_kernel, dm), out_shape=[shape(...  108 us
    pallas_call x1, Pallas kernels, step(): pl.pallas_call(functools.partial(forward_kernel, dm, extra), out_shape=[s...  76.1 us
    pallas_call x1, Pallas kernels, step(): pl.pallas_call(functools.partial(optimizer_kernel, dm), out_shape=[shape(...  18.4 us

profile of v1, /device:TPU:112, one launch (start us, length us, event | category | flops | bytes accessed | tf_op | source)
XLA Modules:
  0.0 348.2 jit_solution(10736511205491023178)
XLA Ops:
  0.6 76.1 %forward.1 = (f32[4,4096,512]{2,1,0:T(8,128)}, f32[4,4096,512]{2,1,0:T(8,128)}, bf16[4096,640]{1,0:T(8,128)(2,1)}, bf16[640,4096]{1,0:T(8,128)(2,1)}, bf16[640,4...) custom-call(bf16[4096,640]{1,0:T(8,128)(2,1)} %bitcast.4, ...), custom_call_target="tpu_custom_call" | custom-call | tf_op jit(solution)/shard_map/forward/pallas_call | solution.py:739
  76.8 144.8 %backward1.1 = (bf16[4,2,240,512]{3,2,1,0:T(8,128)(2,1)}, f32[8,128]{1,0:T(8,128)}, bf16[4096,640]{1,0:T(8,128)(2,1)}, bf16[640,4096]{1,0:T(8,128)(2,1)}, bf16[4...) custom-call(bf16[4096,640]{1,0:T(8,128)(2,1)} %get-tuple-element.24.a1, bf16[640,4096]{1,0:T(8,128)(2,1)} %get-tuple-element.25.a1t, ...), custom_call_target="tpu_custom_call" | custom-call | tf_op jit(solution)/shard_map/backward1/pallas_call | solution.py:759
  221.6 108.0 %backward0.1 = (bf16[2,4,2,240,512]{4,3,2,1,0:T(8,128)(2,1)}, f32[8,128]{1,0:T(8,128)}) custom-call(bf16[4096,640]{1,0:T(8,128)(2,1)} %get-tuple-element.29.dh, bf16[640,4096]{1,0:T(8,128)(2,1)} %get-tuple-element.30.dht, bf16[640,4096]{1,0:T(8,128)(2,1)} %get-tuple-element.31.a0t, f32[4,4096,512]{2,1,0:T(8,128)} %get-tuple-element.32.gates, ...), custom_call_target="tpu_custom_call" | custom-call | tf_op jit(solution)/shard_map/backward0/pallas_call | solution.py:781
  329.6 18.4 %optimizer.1 = (bf16[2,160,2048]{2,1,0:T(8,128)(2,1)}, bf16[2,160,2048]{2,1,0:T(8,128)(2,1)}, bf16[2,512,640]{2,1,0:T(8,128)(2,1)}, f32[2,160,2048]{2,1,0:T(8,12...) custom-call(f32[8,128]{1,0:T(8,128)} %get-tuple-element.37.total, ...), custom_call_target="tpu_custom_call" | custom-call | tf_op jit(solution)/shard_map/optimizer/pallas_call | solution.py:801

commit v2 on v1

v2 whole, which is shorter than its diff:
```python
import dataclasses
import functools

import jax
import jax.numpy as jnp
from jax import lax
from jax.experimental import pallas as pl
from jax.experimental.pallas import tpu as pltpu
from jax.sharding import PartitionSpec as P

BF, F32 = jnp.bfloat16, jnp.float32
LANES = 128
TILE = 1024
SMALL = 512
HALF = 256
VMEM_LIMIT = 67043328
NT = (((1,), (1,)), ((), ()))
NN = (((1,), (0,)), ((), ()))


@dataclasses.dataclass(frozen=True)
class Dims:
    layers: int
    tokens: int
    d: int
    ff: int
    n: int

    @property
    def own_ff(self):
        return self.ff // self.n

    @property
    def rows(self):
        return self.d // self.n

    @property
    def chunk(self):
        return self.n * LANES

    @property
    def chunks(self):
        return self.own_ff // LANES

    @property
    def tiles(self):
        return self.tokens // TILE

    @property
    def small(self):
        return self.tokens // SMALL

    @property
    def packed(self):
        return self.rows + self.d // 2 // self.n


def dot(a, b, dims=NN):
    return lax.dot_general(a, b, dims, preferred_element_type=F32)


def sliced(i, size):
    return pl.ds(pl.multiple_of(i * size, size), size)


def ring(n):
    me = lax.axis_index("dp")
    return me, lax.rem(me + 1, n), lax.rem(me + n - 1, n)


def partner():
    rep = lax.axis_index("rep")
    core = lax.rem(rep, 2)
    return core, rep + 1 - 2 * core


def greet(*others):
    for other in others:
        pl.semaphore_signal(pltpu.get_barrier_semaphore(), inc=1, device_id=other, device_id_type=pl.DeviceIdType.MESH)


def greeted(count):
    pl.semaphore_wait(pltpu.get_barrier_semaphore(), count)


def remote(src, dst, send, recv, device):
    return pltpu.make_async_remote_copy(src_ref=src, dst_ref=dst, send_sem=send, recv_sem=recv, device_id=device, device_id_type=pl.DeviceIdType.MESH)


class Gather:
    COPIES = 14

    def __init__(self, dm, w, sends, recvs):
        self.dm, self.w, self.sends, self.recvs = dm, w, sends, recvs
        self.me, self.right, self.left = ring(dm.n)
        self.far = lax.rem(self.me + 2, dm.n)
        self.core, self.other = partner()

    def _both(self, unit, source):
        half = self.dm.rows // 2
        at = pl.multiple_of(source * self.dm.rows + self.core * half, half)
        return self.w.at[unit, 0:2, pl.ds(at, half), :]

    def _one(self, unit, which, source):
        half = self.dm.rows // 2
        at = pl.multiple_of(source * self.dm.rows + self.core * half, half)
        return self.w.at[unit, which, pl.ds(at, half), :]

    def _down(self, unit, source, quarter=None):
        half = self.dm.d // 2
        columns = pl.ds(pl.multiple_of(source * LANES, LANES), LANES)
        if quarter is None:
            return self.w.at[unit, 2, pl.ds(pl.multiple_of(self.core * half, half), half), columns]
        return self.w.at[unit, 2, pl.ds(pl.multiple_of(self.core * half + quarter * (half // 2), half // 2), half // 2), columns]

    def _copy(self, unit, index, ref, device):
        return remote(ref, ref, self.sends.at[unit, index], self.recvs.at[unit, index], device)

    def own(self, unit, part):
        ref = self._down(unit, self.me) if part else self._both(unit, self.me)
        return [self._copy(unit, 2 * to + part, ref, device) for to, device in enumerate(({"dp": self.right}, {"dp": self.left}))]

    def relayed(self, unit, part):
        if part:
            right, left = self._down(unit, self.left, 0), self._down(unit, self.right, 1)
        else:
            right, left = self._one(unit, 0, self.left), self._one(unit, 1, self.right)
        return [self._copy(unit, 4 + part, right, {"dp": self.right}), self._copy(unit, 6 + part, left, {"dp": self.left})]

    def shared(self, unit, part, sources):
        out = []
        for s in sources:
            source = (self.left, self.right, self.far)[s]
            ref = self._down(unit, source) if part else self._both(unit, source)
            out.append(self._copy(unit, 8 + 2 * s + part, ref, {"rep": self.other}))
        return out

    def _arrivals(self, unit, index, ref):
        return remote(ref, ref, self.sends.at[unit, index], self.recvs.at[unit, index], {"dp": self.right})

    def step1(self, unit, parts=(0, 1)):
        for part in parts:
            for copy in self.own(unit, part):
                copy.start()

    def step2(self, unit):
        for part in range(2):
            for to, source in enumerate((self.left, self.right)):
                ref = self._down(unit, source) if part else self._both(unit, source)
                self._arrivals(unit, 2 * to + part, ref).wait_recv()
            for copy in self.relayed(unit, part) + self.shared(unit, part, (0, 1)):
                copy.start()

    def step3(self, unit):
        for part in range(2):
            for k in range(2):
                ref = self._down(unit, self.far, k) if part else self._one(unit, k, self.far)
                self._arrivals(unit, 4 + 2 * k + part, ref).wait_recv()
            for copy in self.shared(unit, part, (2,)):
                copy.start()

    def _theirs(self, unit, s):
        dm, other = self.dm, 1 - self.core
        source = (self.left, self.right, self.far)[s]
        half = dm.rows // 2
        at = pl.multiple_of(source * dm.rows + other * half, half)
        columns = pl.ds(pl.multiple_of(source * LANES, LANES), LANES)
        rows = pl.ds(pl.multiple_of(other * (dm.d // 2), dm.d // 2), dm.d // 2)
        return self.w.at[unit, 0:2, pl.ds(at, half), :], self.w.at[unit, 2, rows, columns]

    def done(self, unit):
        for s in range(3):
            both, down = self._theirs(unit, s)
            self._arrivals(unit, 8 + 2 * s, both).wait_recv()
            self._arrivals(unit, 9 + 2 * s, down).wait_recv()

    def drain(self, unit):
        for part in range(2):
            for copy in self.own(unit, part) + self.relayed(unit, part) + self.shared(unit, part, (0, 1, 2)):
                copy.wait_send()


def fetch_own(dm, layer, chunk, unit, me, w, sources, sem):
    for which in range(2):
        for q in range(dm.n):
            pltpu.make_async_copy(
                sources[which].at[layer, :, pl.ds(q * dm.own_ff + chunk * LANES, LANES)],
                w.at[unit, which, sliced(me, dm.rows), pl.ds(q * LANES, LANES)],
                sem,
            ).start()


def await_own(dm, unit, me, w, sem):
    ref = w.at[unit, 0:2, sliced(me, dm.rows), :]
    pltpu.make_async_copy(ref, ref, sem).wait()


def scale_of(wide, axis, count):
    return lax.rsqrt(jnp.sum(wide * wide, axis, keepdims=True) / count + 1e-6)


def move(src, dst, sem):
    return pltpu.make_async_copy(src, dst, sem)


def forward_kernel(
    dm, extra, x, dy, w_gate, w_up, w_down,
    gates, ups, acts, a1, a1t, h1t, a0t, dyt, wd0, w1,
    abuf, xt, at, ht, w, gst, ust, ast, natural, dyb, dytb,
    own_sem, nat_sem, x_sem, dy_sem, dyt_sem, st_sem, at_sem, out_sem, w_sem, sends, recvs,
):
    tiles, units = dm.tiles, dm.chunks + extra
    gather = Gather(dm, w, sends, recvs)
    me = gather.me
    place = lambda u: (u // dm.chunks, u % dm.chunks)
    greet({"dp": gather.right}, {"dp": gather.left}, {"rep": gather.other})
    fetch_own(dm, *place(0), 0, me, w, (w_gate, w_up), own_sem.at[0])
    move(w_down.at[0], natural.at[0], nat_sem.at[0]).start()
    for t in range(dm.small):
        move(x.at[pl.ds(t * SMALL, SMALL), :], abuf.at[pl.ds(t * SMALL, SMALL), :], x_sem.at[t]).start()
    await_own(dm, 0, me, w, own_sem.at[0])
    greeted(3)
    gather.step1(0, (0,))
    columns = pl.ds(pl.multiple_of(me * LANES, LANES), LANES)
    move(w_down.at[0], natural.at[0], nat_sem.at[0]).wait()
    w[0, 2, :, columns] = natural[0, 0:LANES, :].T
    gather.step1(0, (1,))
    for u in range(1, units):
        fetch_own(dm, *place(u), u, me, w, (w_gate, w_up), own_sem.at[u])
    move(w_down.at[1], natural.at[1], nat_sem.at[1]).start()
    for t in range(dm.small):
        move(dy.at[pl.ds(t * SMALL, SMALL), :], dyb.at[pl.ds(t * SMALL, SMALL), :], dy_sem.at[t]).start()

    @pl.loop(0, dm.small)
    def _(t):
        at_t = sliced(t, SMALL)
        move(x.at[at_t, :], abuf.at[at_t, :], x_sem.at[t]).wait()
        tile = abuf[at_t, :]
        wide = tile.astype(F32)
        a = (wide * scale_of(wide, -1, dm.d)).astype(BF)
        xt[:, at_t] = tile.T
        at[:, at_t] = a.T
        abuf[at_t, :] = a

    gather.step2(0)
    move(w_down.at[1], natural.at[1], nat_sem.at[1]).wait()
    for u in range(1, units):
        layer, chunk = place(u)
        w[u, 2, :, columns] = natural[layer, pl.ds(chunk * LANES, LANES), :].T
    await_own(dm, 1, me, w, own_sem.at[1])
    gather.step1(1)
    move(at, a0t, at_sem.at[0]).start()

    @pl.loop(0, dm.small)
    def _(t):
        at_t = sliced(t, SMALL)
        move(dy.at[at_t, :], dyb.at[at_t, :], dy_sem.at[t]).wait()
        dytb[:, at_t] = dyb[at_t, :].T

    move(dytb, dyt, dyt_sem.at[0]).start()
    gather.step3(0)

    def stored(i):
        slot, chunk, at_t = lax.rem(i, 2), i // tiles, sliced(lax.rem(i, tiles), TILE)
        pairs = ((gst, gates), (ust, ups), (ast, acts))
        return [move(a.at[slot], b.at[chunk, at_t, :], st_sem.at[k, slot]) for k, (a, b) in enumerate(pairs)]

    def results(t):
        at_t = sliced(t, TILE)
        return (
            move(abuf.at[at_t, :], a1.at[at_t, :], out_sem.at[0, t]),
            move(at.at[:, at_t], a1t.at[:, at_t], out_sem.at[1, t]),
            move(xt.at[:, at_t], h1t.at[:, at_t], out_sem.at[2, t]),
        )

    def tile_step(i, last):
        c, t = i // tiles, lax.rem(i, tiles)
        slot, at_t = lax.rem(i, 2), sliced(t, TILE)

        @pl.when(t == 0)
        def _():
            gather.done(c)
            if last:
                move(w.at[0 : dm.chunks, 2], wd0, w_sem.at[0]).start()

        @pl.when(t == 1)
        def _():
            gather.step2(c + 1)

        @pl.when(t == 1 if not last else t == 2)
        def _():
            if last:
                gather.step2(c + 2)
            else:
                await_own(dm, c + 2, me, w, own_sem.at[c + 2])
                gather.step1(c + 2)

        @pl.when(t == 3)
        def _():
            gather.step3(c + 1)

        if not last:

            @pl.when(i == (dm.chunks - 1) * tiles - 1)
            def _():
                await_own(dm, units - 1, me, w, own_sem.at[units - 1])
                gather.step1(units - 1)

        @pl.when(i >= 1)
        def _():
            for copy in stored(i - 1):
                copy.start()

        @pl.when(i >= 2)
        def _():
            for copy in stored(i - 2):
                copy.wait()

        if last:

            @pl.when(t >= 1)
            def _():
                for copy in results(t - 1):
                    copy.start()

        a = abuf[at_t, :]
        for b in range(0, dm.chunk, HALF):
            part = slice(b, b + HALF)
            gate = dot(a, w[c, 0, :, part])
            up = dot(a, w[c, 1, :, part])
            gst[slot, :, part] = gate
            ust[slot, :, part] = up
            ast[slot, :, part] = (gate * jax.nn.sigmoid(gate) * up).astype(BF)
        if not last:
            ht[:, at_t] = jnp.where(c == 0, 0.0, ht[:, at_t]) + dot(w[c, 2], ast[slot], NT)
            return
        for b in range(0, TILE, HALF):
            at_b = pl.ds(pl.multiple_of(t * TILE + b, HALF), HALF)
            total = ht[:, at_b] + dot(w[c, 2], ast[slot, b : b + HALF, :], NT)
            h = xt[:, at_b] + total.astype(BF)
            wide = h.astype(F32)
            a = (wide * scale_of(wide, 0, dm.d)).astype(BF)
            xt[:, at_b] = h
            at[:, at_b] = a
            abuf[at_b, :] = a.T

    steps = dm.chunks * tiles

    @pl.loop(0, steps - tiles)
    def _(i):
        tile_step(i, False)

    move(at, a0t, at_sem.at[0]).wait()

    @pl.loop(steps - tiles, steps)
    def _(i):
        tile_step(i, True)

    for copy in (*stored(steps - 1), *results(tiles - 1)):
        copy.start()
    gather.step3(units - 1)
    for u in range(dm.chunks, units):
        gather.done(u)
    move(w.at[dm.chunks : units], w1, w_sem.at[1]).start()
    for i in range(steps - 2, steps):
        for copy in stored(i):
            copy.wait()
    for t in range(tiles):
        for copy in results(t):
            copy.wait()
    move(w.at[0 : dm.chunks, 2], wd0, w_sem.at[0]).wait()
    move(w.at[dm.chunks : units], w1, w_sem.at[1]).wait()
    move(dytb, dyt, dyt_sem.at[0]).wait()
    for u in range(units):
        gather.drain(u)


class Scatter:
    def __init__(self, dm, wide, acc, send, recv, sends, recvs):
        self.dm, self.wide, self.acc, self.send, self.recv, self.sends, self.recvs = dm, wide, acc, send, recv, sends, recvs
        self.me, self.right, self.left = ring(dm.n)
        self.far = lax.rem(self.me + 2, dm.n)

    def _copy(self, c, kind):
        device = {"dp": self.right if kind % 2 == 0 else self.left}
        s, r = lax.rem(c, self.send.shape[0]), lax.rem(c, self.recv.shape[0])
        return remote(self.send.at[s, kind], self.recv.at[r, kind], self.sends.at[s, kind], self.recvs.at[r, kind], device)

    def _parts(self, c, owner, half):
        dm, slot = self.dm, lax.rem(c, self.acc.shape[0])
        if self.wide:
            return [(self.acc[slot, half, sliced(owner, dm.rows), :], slice(None))]
        columns = pl.ds(pl.multiple_of(owner * LANES, LANES), LANES)
        size = dm.d // 2 // dm.n
        return [
            (self.acc[slot, pl.ds(half * (dm.d // 2) + i * size, size), columns], slice(i * LANES, (i + 1) * LANES)) for i in range(dm.n)
        ]

    def _put(self, c, kind, owner, half, add=None):
        s, r = lax.rem(c, self.send.shape[0]), lax.rem(c, self.recv.shape[0])
        for term, columns in self._parts(c, owner, half):
            if add is not None:
                term = term + self.recv[r, add, :, columns].astype(F32)
            self.send[s, kind, :, columns] = term.astype(BF)
        self._copy(c, kind).start()

    def step1(self, c):
        self._put(c, 0, self.far, 0)
        self._put(c, 1, self.far, 1)
        self._put(c, 2, self.right, 1)
        self._put(c, 3, self.left, 0)

    def step2(self, c):
        for kind, owner, half in ((0, self.right, 0), (1, self.left, 1)):
            self._copy(c, kind).wait_recv()
            self._put(c, kind + 4, owner, half, add=kind)
        for kind in (0, 1):
            self._copy(c, kind).wait_send()

    def step3(self, c, put, squares):
        for kind in (2, 3, 4, 5):
            self._copy(c, kind).wait_recv()
        r = lax.rem(c, self.recv.shape[0])
        for half, kinds in ((0, (4, 3)), (1, (2, 5))):
            for term, columns in self._parts(c, self.me, half):
                for kind in kinds:
                    term = term + self.recv[r, kind, :, columns].astype(F32)
                g = term.astype(BF)
                put(half, columns, g)
                g = g.astype(F32)
                g = jnp.sum((g * g).reshape(-1, 8, g.shape[-1]), 0)
                for j in range(0, g.shape[-1], LANES):
                    squares[...] += g[:, j : j + LANES]
        for kind in (2, 3, 4, 5):
            self._copy(c, kind).wait_send()


def back_through(gate, up, by_act):
    by_act = by_act.astype(BF).astype(F32)
    s = jax.nn.sigmoid(gate)
    by_up = (by_act * (gate * s)).astype(BF)
    by_gate = (by_act * up * (s * (1.0 + gate * (1.0 - s)))).astype(BF)
    return by_gate, by_up


def backward1_kernel(
    dm, a1, a1t, dy, dyt, h1t, w_gate, w_up, w_down, w1,
    grads_out, squares_out, dh, dht, by_gates, by_ups,
    abuf, at, dyb, dytb, w, natural, wacc, dacc, ba, bg, bu, stash, hb, dhb, dhtb, wsend, wrecv, dsend, drecv, grads, squares,
    own_sem, nat_sem, w_sem, in_sem, b_sem, b2_sem, h_sem, o_sem, g_sem, sends, recvs, wsends, wrecvs, dsends, drecvs,
):
    tiles, small, units = dm.tiles, dm.small, dm.chunks
    gather = Gather(dm, w, sends, recvs)
    wides = Scatter(dm, True, wacc, wsend, wrecv, wsends, wrecvs)
    downs = Scatter(dm, False, dacc, dsend, drecv, dsends, drecvs)
    me, layer, known = gather.me, 1, w1.shape[0]
    loads = lambda t: (
        move(a1.at[sliced(t, TILE), :], abuf.at[sliced(t, TILE), :], in_sem.at[0, t]),
        move(dy.at[sliced(t, TILE), :], dyb.at[sliced(t, TILE), :], in_sem.at[1, t]),
        move(a1t.at[:, sliced(t, TILE)], at.at[:, sliced(t, TILE)], in_sem.at[2, t]),
        move(dyt.at[:, sliced(t, TILE)], dytb.at[:, sliced(t, TILE)], in_sem.at[3, t]),
    )
    greet({"dp": gather.right}, {"dp": gather.left}, {"rep": gather.other})
    move(w_down.at[layer], natural, nat_sem.at[0]).start()
    for u in range(known, units):
        fetch_own(dm, layer, u, u, me, w, (w_gate, w_up), own_sem.at[u])
    move(w1.at[0], w.at[0], w_sem.at[0]).start()
    for copy in loads(0):
        copy.start()
    for u in range(1, known):
        move(w1.at[u], w.at[u], w_sem.at[u]).start()
    squares[...] = jnp.zeros_like(squares)
    move(w_down.at[layer], natural, nat_sem.at[0]).wait()
    columns = pl.ds(pl.multiple_of(me * LANES, LANES), LANES)
    for u in range(known, units):
        w[u, 2, :, columns] = natural[pl.ds(u * LANES, LANES), :].T
    for u in range(known, units):
        await_own(dm, u, me, w, own_sem.at[u])
    greeted(3)
    gather.step1(known)
    for t in range(1, tiles):
        for copy in loads(t):
            copy.start()
    move(w1.at[0], w.at[0], w_sem.at[0]).wait()

    def stored(i):
        slot, chunk, at_t = lax.rem(i, 2), i // tiles, sliced(lax.rem(i, tiles), TILE)
        return [move(a.at[slot], b.at[chunk, at_t, :], b_sem.at[k, slot]) for k, (a, b) in enumerate(((bg, by_gates), (bu, by_ups)))]

    def step1(c):
        wides.step1(c)
        downs.step1(c)

    def step2(c):
        wides.step2(c)
        downs.step2(c)

    def step3(c):
        def put(first, last):
            def put(half, columns, g):
                grads[c, half, first:last, columns] = g

            return put

        wides.step3(c, put(0, dm.rows), squares)
        downs.step3(c, put(dm.rows, dm.packed), squares)

    def inputs(t):
        slot, third, at_t = lax.rem(t, 2), lax.rem(t, 3), sliced(t, SMALL)
        out = [move(h1t.at[:, at_t], hb.at[third], h_sem.at[third])]
        for k, (src, dst) in enumerate(((by_gates, abuf), (by_ups, dyb))):
            for c in range(dm.chunks):
                out.append(move(src.at[c, at_t, :], dst.at[sliced(slot * dm.chunks + c, SMALL), 0 : dm.chunk], b2_sem.at[k, slot, c]))
        return out

    steps = dm.chunks * tiles

    @pl.loop(0, steps)
    def _(i):
        c, t = i // tiles, lax.rem(i, tiles)
        slot, at_t = lax.rem(i, 2), sliced(t, TILE)

        @pl.when(c == 0)
        def _():
            for copy in loads(t):
                copy.wait()

        @pl.when(jnp.logical_and(t == 0, c >= 2))
        def _():
            gather.done(c)
            step3(c - 2)

        @pl.when(jnp.logical_and(t == 0, c >= 1))
        def _():
            step1(c - 1)

        @pl.when(i == 2)
        def _():
            gather.step2(known)
            gather.step1(known + 1)

        @pl.when(i == 3)
        def _():
            for u in range(1, known):
                move(w1.at[u], w.at[u], w_sem.at[u]).wait()
            gather.step3(known)

        @pl.when(i == 5)
        def _():
            gather.step2(known + 1)

        @pl.when(i == 7)
        def _():
            gather.step3(known + 1)

        @pl.when(jnp.logical_and(t == 2, c >= 1))
        def _():
            step2(c - 1)

        @pl.when(i >= 1)
        def _():
            for copy in stored(i - 1):
                copy.start()

        @pl.when(i >= 2)
        def _():
            for copy in stored(i - 2):
                copy.wait()

        @pl.when(i == steps - 1)
        def _():
            for copy in inputs(0):
                copy.start()

        a, y = abuf[at_t, :], dyb[at_t, :]
        for b in range(0, dm.chunk, HALF):
            part = slice(b, b + HALF)
            gate, up = dot(a, w[c, 0, :, part]), dot(a, w[c, 1, :, part])
            by_gate, by_up = back_through(gate, up, dot(y, w[c, 2, :, part]))
            ba[:, part] = (gate * jax.nn.sigmoid(gate) * up).astype(BF)
            bg[slot, :, part] = by_gate
            bu[slot, :, part] = by_up
        s = lax.rem(c, 2)
        wacc[s, 0] = jnp.where(t == 0, 0.0, wacc[s, 0]) + dot(at[:, at_t], bg[slot])
        wacc[s, 1] = jnp.where(t == 0, 0.0, wacc[s, 1]) + dot(at[:, at_t], bu[slot])
        dacc[s] = jnp.where(t == 0, 0.0, dacc[s]) + dot(dytb[:, at_t], ba[...])

    last = dm.chunks - 1
    for copy in stored(steps - 1):
        copy.start()
    step3(last - 1)
    step1(last)
    for i in range(steps - 2, steps):
        for copy in stored(i):
            copy.wait()

    def results(t):
        slot, at_t = lax.rem(t, 2), sliced(t, SMALL)
        return (
            move(dhb.at[slot], dh.at[at_t, :], o_sem.at[0, slot]),
            move(dhtb.at[slot], dht.at[:, at_t], o_sem.at[1, slot]),
        )

    def matmuls(t):
        slot, total = lax.rem(t, 2), None
        for c in range(dm.chunks):
            rows = sliced(slot * dm.chunks + c, SMALL)
            term = dot(w[c, 0], abuf[rows, 0 : dm.chunk], NT) + dot(w[c, 1], dyb[rows, 0 : dm.chunk], NT)
            total = term if total is None else total + term
        return total.astype(BF)

    def finish(t, by_a):
        slot, at_t = lax.rem(t, 2), sliced(t, SMALL)
        by_a = by_a.astype(F32)
        h = hb[lax.rem(t, 3)].astype(F32)
        square = jnp.sum(h * h, 0, keepdims=True) / dm.d + 1e-6
        scale = lax.rsqrt(square)
        along = jnp.sum(h * by_a, 0, keepdims=True) * (scale / square) / dm.d
        by_h = dytb[:, at_t] + (by_a * scale - h * along).astype(BF)
        dhtb[slot] = by_h
        dhb[slot] = by_h.T

    for copy in inputs(1):
        copy.start()
    for copy in inputs(0):
        copy.wait()
    stash[...] = matmuls(0)

    @pl.loop(1, small)
    def _(t):
        @pl.when(t >= 2)
        def _():
            for copy in results(t - 2):
                copy.start()

        @pl.when(t == 3)
        def _():
            step2(last)

        @pl.when(t == 6)
        def _():
            step3(last)

        for copy in inputs(t):
            copy.wait()

        @pl.when(t + 1 < small)
        def _():
            for copy in inputs(t + 1):
                copy.start()

        @pl.when(t >= 3)
        def _():
            for copy in results(t - 3):
                copy.wait()

        finish(t - 1, stash[...])
        stash[...] = matmuls(t)

    for copy in results(small - 2):
        copy.start()
    for copy in results(small - 3):
        copy.wait()
    finish(small - 1, stash[...])
    for copy in results(small - 1):
        copy.start()
    for t in (small - 2, small - 1):
        for copy in results(t):
            copy.wait()
    for u in range(known, units):
        gather.drain(u)
    move(grads, grads_out, g_sem.at[0]).start()
    move(squares, squares_out, g_sem.at[1]).start()
    move(grads, grads_out, g_sem.at[0]).wait()
    move(squares, squares_out, g_sem.at[1]).wait()


def backward0_kernel(
    dm, dh, dht, a0t, gates, ups, acts, wd0, grads1, squares1,
    grads_out, total_out,
    dhb, dhtb, at, wd, ab, gb, ub, bg, bu, wacc, dacc, wsend, wrecv, dsend, drecv, grads, squares, everyone,
    in_sem, w_sem, a_sem, gu_sem, g_sem, wsends, wrecvs, dsends, drecvs, ssends, srecvs,
):
    halves, cuts = 2, dm.chunk // HALF
    wides = Scatter(dm, True, wacc, wsend, wrecv, wsends, wrecvs)
    downs = Scatter(dm, False, dacc, dsend, drecv, dsends, drecvs)
    me, span = wides.me, dm.tokens // halves
    greet({"dp": wides.right}, {"dp": wides.left}, {"dp": wides.far})

    def hidden(i):
        slot = lax.rem(i, 2)
        return move(acts.at[i // halves, sliced(lax.rem(i, halves), span), :], ab.at[slot], a_sem.at[slot])

    def inputs(i):
        slot, unit, at_t = lax.rem(i, 2), i // halves, sliced(lax.rem(i, halves), span)
        columns = pl.ds(pl.multiple_of(lax.rem(unit, cuts) * HALF, HALF), HALF)
        return (
            move(gates.at[unit // cuts, at_t, columns], gb.at[slot], gu_sem.at[0, slot]),
            move(ups.at[unit // cuts, at_t, columns], ub.at[slot], gu_sem.at[1, slot]),
        )

    firsts = [move(dht.at[:, pl.ds(k * span, span)], dhtb.at[:, pl.ds(k * span, span)], in_sem.at[k]) for k in range(halves)]
    rest = [move(dh, dhb, in_sem.at[2]), move(a0t, at, in_sem.at[3]), move(wd0, wd, w_sem.at[0])]
    firsts[0].start()
    hidden(0).start()
    firsts[1].start()
    hidden(1).start()
    move(squares1, squares, g_sem.at[1]).start()
    @pl.loop(0, dm.chunks * halves)
    def _(i):
        c, t = i // halves, lax.rem(i, halves)
        for k in range(halves):

            @pl.when(i == k)
            def _():
                firsts[k].wait()

        @pl.when(i == 1)
        def _():
            greeted(3)

        @pl.when(jnp.logical_and(i >= 1, i + 1 < dm.chunks * halves))
        def _():
            hidden(i + 1).start()

        @pl.when(i == 2)
        def _():
            for copy in rest:
                copy.start()

        @pl.when(i == 5)
        def _():
            for copy in (*inputs(0), *inputs(1), move(grads1, grads.at[1], g_sem.at[0])):
                copy.start()

        hidden(i).wait()
        dacc[c] = jnp.where(t == 0, 0.0, dacc[c]) + dot(dhtb[:, sliced(t, span)], ab[lax.rem(i, 2)])

        @pl.when(t == halves - 1)
        def _():
            downs.step1(c)

    for copy in rest:
        copy.wait()
    move(squares1, squares, g_sem.at[1]).wait()

    def put_down(c):
        def put(half, columns, g):
            grads[0, c, half, dm.rows : dm.packed, columns] = g

        return put

    def put_wide(unit):
        def put(half, columns, g):
            grads[0, unit // cuts, half, 0 : dm.rows, pl.ds(pl.multiple_of(lax.rem(unit, cuts) * HALF, HALF), HALF)] = g

        return put

    units = dm.chunks * cuts
    steps = units * halves

    @pl.loop(0, steps)
    def _(i):
        unit, t = i // halves, lax.rem(i, halves)
        slot = lax.rem(i, 2)

        @pl.when(jnp.logical_and(t == 0, unit >= 1))
        def _():
            wides.step1(unit - 1)

        @pl.when(jnp.logical_and(t == 1, unit >= 2))
        def _():
            wides.step2(unit - 2)

        @pl.when(jnp.logical_and(t == 1, unit >= 3))
        def _():
            wides.step3(unit - 3, put_wide(unit - 3), squares)

        @pl.when(i < dm.chunks)
        def _():
            downs.step2(i)

        @pl.when(jnp.logical_and(i >= dm.chunks, i < 2 * dm.chunks))
        def _():
            downs.step3(i - dm.chunks, put_down(i - dm.chunks), squares)

        @pl.when(jnp.logical_and(i >= 1, i + 1 < steps))
        def _():
            for copy in inputs(i + 1):
                copy.start()

        for copy in inputs(i):
            copy.wait()
        weights = wd[unit // cuts, :, pl.ds(pl.multiple_of(lax.rem(unit, cuts) * HALF, HALF), HALF)]
        blocks = [(slice(b, b + SMALL), sliced(t * (span // SMALL) + b // SMALL, SMALL)) for b in range(0, span, SMALL)]
        by_acts = [dot(dhb[tokens, :], weights) for _, tokens in blocks]
        totals = [None, None]
        for (rows, tokens), by_act in zip(blocks, by_acts, strict=True):
            bg[rows, :], bu[rows, :] = back_through(gb[slot, rows, :], ub[slot, rows, :], by_act)
            for which, right in enumerate((bg, bu)):
                term = dot(at[:, tokens], right[rows, :])
                totals[which] = term if totals[which] is None else totals[which] + term
        s = lax.rem(unit, wacc.shape[0])
        for which in range(2):
            wacc[s, which] = jnp.where(t == 0, 0.0, wacc[s, which]) + totals[which]

    last = units - 1
    wides.step1(last)
    wides.step2(last - 1)
    wides.step3(last - 2, put_wide(last - 2), squares)
    wides.step2(last)
    wides.step3(last - 1, put_wide(last - 1), squares)
    wides.step3(last, put_wide(last), squares)
    move(grads1, grads.at[1], g_sem.at[0]).wait()
    move(grads, grads_out, g_sem.at[2]).start()

    copies = []
    for k in range(1, dm.n):
        to = lax.rem(me + k, dm.n)
        copies.append(remote(squares, everyone.at[me], ssends.at[k - 1], srecvs.at[k - 1], {"dp": to}))
    for copy in copies:
        copy.start()
    everyone[me] = squares[...]
    for copy in copies:
        copy.wait()
    total = everyone[0]
    for k in range(1, dm.n):
        total = total + everyone[k]
    total_out[...] = total
    move(grads, grads_out, g_sem.at[2]).wait()


def optimizer_kernel(dm, total, grads, *refs):
    ins, outs = refs[:9], refs[9:]
    count = dm.layers * 3 * dm.d * dm.ff
    factor = jnp.minimum(1.0, 0.5 * lax.rsqrt(jnp.sum(total[...]) / count + 1e-30))
    layer, q = pl.program_id(0), pl.program_id(1)
    size = dm.d // 2 // dm.n
    wide = [
        jnp.concatenate([grads[layer, c, half, 0 : dm.rows, pl.ds(pl.multiple_of(q * LANES, LANES), LANES)] for c in range(dm.chunks)], axis=1)
        for half in range(2)
    ]
    down = jnp.concatenate(
        [grads[layer, q, half, dm.rows : dm.packed, i * LANES : (i + 1) * LANES] for half in range(2) for i in range(dm.n)], axis=0
    ).T
    for which, g in enumerate((*wide, down)):
        w, m, v = (ins[which + 3 * j][0] for j in range(3))
        g = g.astype(F32) * factor
        w = w.astype(F32)
        m = 0.9 * m + 0.1 * g
        v = 0.95 * v + 0.05 * g * g
        step = m * lax.rsqrt(v + 1e-8) + 0.1 * w
        outs[which][0] = (w - 0.02 * step).astype(BF)
        outs[which + 3][0] = m
        outs[which + 6][0] = v


def step(mesh, x, dy, *arrays):
    weights, m, v = (arrays[i : i + 3] for i in (0, 3, 6))
    x, dy = x[0], dy[0]
    w_gate, w_up, w_down = weights
    n = mesh.shape["dp"]
    dm = Dims(w_gate.shape[0], x.shape[0], x.shape[1], w_gate.shape[2], n)
    tokens, d, chunk, chunks, tiles = dm.tokens, dm.d, dm.chunk, dm.chunks, dm.tiles
    hbm = pl.BlockSpec(memory_space=pltpu.HBM)
    vmem = pl.BlockSpec(memory_space=pltpu.VMEM)
    shape = jax.ShapeDtypeStruct
    dma = lambda *s: pltpu.SemaphoreType.DMA(s)
    params = lambda i: pltpu.CompilerParams(vmem_limit_bytes=VMEM_LIMIT, collective_id=i, has_side_effects=True)
    natural, turned = (tokens, d), (d, tokens)

    extra = 2
    units = chunks + extra
    per_chunk = (chunks, tokens, chunk)
    gates, ups, acts, a1, a1t, h1t, a0t, dyt, wd0, w1 = pl.pallas_call(
        functools.partial(forward_kernel, dm, extra),
        out_shape=[
            shape(per_chunk, F32), shape(per_chunk, F32), shape(per_chunk, BF), shape(natural, BF), shape(turned, BF), shape(turned, BF),
            shape(turned, BF), shape(turned, BF), shape((chunks, d, chunk), BF), shape((extra, 3, d, chunk), BF),
        ],
        in_specs=[hbm] * 5,
        out_specs=[hbm] * 10,
        scratch_shapes=[
            pltpu.VMEM(natural, BF), pltpu.VMEM(turned, BF), pltpu.VMEM(turned, BF), pltpu.VMEM(turned, F32),
            pltpu.VMEM((units, 3, d, chunk), BF), pltpu.VMEM((2, TILE, chunk), F32), pltpu.VMEM((2, TILE, chunk), F32), pltpu.VMEM((2, TILE, chunk), BF),
            pltpu.VMEM((2, dm.own_ff, d), BF), pltpu.VMEM(natural, BF), pltpu.VMEM(turned, BF),
            dma(units), dma(2), dma(dm.small), dma(dm.small), dma(1), dma(3, 2), dma(1), dma(3, tiles), dma(2),
            dma(units, Gather.COPIES), dma(units, Gather.COPIES),
        ],
        compiler_params=params(0),
        name="forward",
    )(x, dy, w_gate, w_up, w_down)

    block = (dm.packed, chunk)
    wide, thin, down = (dm.rows, chunk), (dm.rows, HALF), (dm.packed - dm.rows, chunk)
    grads1, squares1, dh, dht, _, _ = pl.pallas_call(
        functools.partial(backward1_kernel, dm),
        out_shape=[
            shape((chunks, 2, *block), BF), shape((8, LANES), F32), shape(natural, BF), shape(turned, BF), shape(per_chunk, BF), shape(per_chunk, BF),
        ],
        in_specs=[hbm] * 9,
        out_specs=[hbm] * 6,
        scratch_shapes=[
            pltpu.VMEM(natural, BF), pltpu.VMEM(turned, BF), pltpu.VMEM(natural, BF), pltpu.VMEM(turned, BF),
            pltpu.VMEM((chunks, 3, d, chunk), BF), pltpu.VMEM((dm.own_ff, d), BF), pltpu.VMEM((2, 2, d, chunk), F32), pltpu.VMEM((2, d, chunk), F32),
            pltpu.VMEM((TILE, chunk), BF), pltpu.VMEM((2, TILE, chunk), BF), pltpu.VMEM((2, TILE, chunk), BF),
            pltpu.VMEM((d, SMALL), BF), pltpu.VMEM((3, d, SMALL), BF), pltpu.VMEM((2, SMALL, d), BF), pltpu.VMEM((2, d, SMALL), BF),
            pltpu.VMEM((1, 6, *wide), BF), pltpu.VMEM((2, 6, *wide), BF), pltpu.VMEM((1, 6, *down), BF), pltpu.VMEM((2, 6, *down), BF),
            pltpu.VMEM((chunks, 2, *block), BF), pltpu.VMEM((8, LANES), F32),
            dma(chunks), dma(1), dma(extra), dma(4, tiles), dma(2, 2), dma(2, 2, chunks), dma(3), dma(2, 2), dma(2),
            dma(chunks, Gather.COPIES), dma(chunks, Gather.COPIES), dma(1, 6), dma(2, 6), dma(1, 6), dma(2, 6),
        ],
        compiler_params=params(1),
        name="backward1",
    )(a1, a1t, dy, dyt, h1t, w_gate, w_up, w_down, w1)

    grads, total = pl.pallas_call(
        functools.partial(backward0_kernel, dm),
        out_shape=[shape((2, chunks, 2, *block), BF), shape((8, LANES), F32)],
        in_specs=[hbm] * 9,
        out_specs=[hbm, vmem],
        scratch_shapes=[
            pltpu.VMEM(natural, BF), pltpu.VMEM(turned, BF), pltpu.VMEM(turned, BF), pltpu.VMEM((chunks, d, chunk), BF),
            pltpu.VMEM((2, tokens // 2, chunk), BF), pltpu.VMEM((2, tokens // 2, HALF), F32), pltpu.VMEM((2, tokens // 2, HALF), F32),
            pltpu.VMEM((tokens // 2, HALF), BF), pltpu.VMEM((tokens // 2, HALF), BF), pltpu.VMEM((4, 2, d, HALF), F32), pltpu.VMEM((chunks, d, chunk), F32),
            pltpu.VMEM((3, 6, *thin), BF), pltpu.VMEM((5, 6, *thin), BF), pltpu.VMEM((chunks, 6, *down), BF), pltpu.VMEM((chunks, 6, *down), BF),
            pltpu.VMEM((2, chunks, 2, *block), BF), pltpu.VMEM((8, LANES), F32), pltpu.VMEM((n, 8, LANES), F32),
            dma(4), dma(1), dma(2), dma(2, 2), dma(3), dma(3, 6), dma(5, 6), dma(chunks, 6), dma(chunks, 6), dma(n - 1), dma(n - 1),
        ],
        compiler_params=params(2),
        name="backward0",
    )(dh, dht, a0t, gates, ups, acts, wd0, grads1, squares1)

    wide = pl.BlockSpec((1, dm.rows, chunks * LANES), lambda l, q: (l, 0, q))
    down = pl.BlockSpec((1, LANES, d), lambda l, q: (l, q, 0))
    whole = lambda s: pl.BlockSpec(s, lambda l, q: (0,) * len(s))
    return tuple(
        pl.pallas_call(
            functools.partial(optimizer_kernel, dm),
            out_shape=[shape(w.shape, BF) for w in weights] + [shape(w.shape, F32) for w in weights] * 2,
            grid=(dm.layers, dm.n),
            in_specs=[whole((8, LANES)), whole((2, chunks, 2, *block))] + [wide, wide, down] * 3,
            out_specs=[wide, wide, down] * 3,
            compiler_params=pltpu.CompilerParams(dimension_semantics=("arbitrary", "arbitrary")),
            name="optimizer",
        )(total, grads, *weights, *m, *v)
    )


def solution(mesh):
    states, cut = P(("rep", "dp"), None, None), P(None, "dp", None)
    return jax.shard_map(
        functools.partial(step, mesh),
        mesh=mesh,
        in_specs=(states, states) + (cut,) * 9,
        out_specs=(P("rep", "dp", None),) * 9,
        check_vma=False,
    )
```

time: 348 us -> 288 us (0.83)
  Pallas kernels: 347 us -> 287 us
    pallas_call x1, Pallas kernels: 108 us -> 79.8 us  [step(): pl.pallas_call(functools.partial(backward0_kernel, dm), out_shape=[shape(...]
    pallas_call x1, Pallas kernels: 145 us -> 118 us  [step(): pl.pallas_call(functools.partial(backward1_kernel, dm), out_shape=[shape(...]
    pallas_call x1, Pallas kernels: 76.1 us -> 71 us  [step(): pl.pallas_call(functools.partial(forward_kernel, dm, extra), out_shape=[s...]
where the time goes in v2:
time: 288 us
  Pallas kernels  287 us (100%)
    pallas_call x1, Pallas kernels, step(): pl.pallas_call(functools.partial(backward1_kernel, dm), out_shape=[shape(...  118 us
    pallas_call x1, Pallas kernels, step(): pl.pallas_call(functools.partial(backward0_kernel, dm), out_shape=[shape(...  79.8 us
    pallas_call x1, Pallas kernels, step(): pl.pallas_call(functools.partial(forward_kernel, dm, extra), out_shape=[s...  71 us
    pallas_call x1, Pallas kernels, step(): pl.pallas_call(functools.partial(optimizer_kernel, dm), out_shape=[shape(...  18.4 us

profile of v2, /device:TPU:112, one launch (start us, length us, event | category | flops | bytes accessed | tf_op | source)
XLA Modules:
  0.0 288.1 jit_solution(17340500190046341277)
XLA Ops:
  0.6 71.0 %forward.1 = (f32[4,4096,512]{2,1,0:T(8,128)}, f32[4,4096,512]{2,1,0:T(8,128)}, bf16[4,4096,512]{2,1,0:T(8,128)(2,1)}, bf16[4096,640]{1,0:T(8,128)(2,1)}, bf16[6...) custom-call(bf16[4096,640]{1,0:T(8,128)(2,1)} %bitcast.4, ...), custom_call_target="tpu_custom_call" | custom-call | tf_op jit(solution)/shard_map/forward/pallas_call | solution.py:875
  71.6 118.0 %backward1.1 = (bf16[4,2,240,512]{3,2,1,0:T(8,128)(2,1)}, f32[8,128]{1,0:T(8,128)}, bf16[4096,640]{1,0:T(8,128)(2,1)}, bf16[640,4096]{1,0:T(8,128)(2,1)}, bf16[4...) custom-call(bf16[4096,640]{1,0:T(8,128)(2,1)} %get-tuple-element.25.a1, bf16[640,4096]{1,0:T(8,128)(2,1)} %get-tuple-element.26.a1t, ...), custom_call_target="tpu_custom_call" | custom-call | tf_op jit(solution)/shard_map/backward1/pallas_call | solution.py:896
  189.6 79.8 %backward0.1 = (bf16[2,4,2,240,512]{4,3,2,1,0:T(8,128)(2,1)}, f32[8,128]{1,0:T(8,128)}) custom-call(bf16[4096,640]{1,0:T(8,128)(2,1)} %get-tuple-element.30.dh, bf16[640,4096]{1,0:T(8,128)(2,1)} %get-tuple-element.31.dht, bf16[640,4096]{1,0:T(8,128)(2,1)} %get-tuple-element.32.a0t, f32[4,4096,512]{2,1,0:T(8,128)} %get-tuple-element.33.gates, ...), custom_call_target="tpu_custom_call" | custom-call | tf_op jit(solution)/shard_map/backward0/pallas_call | solution.py:917
  269.5 18.4 %optimizer.1 = (bf16[2,160,2048]{2,1,0:T(8,128)(2,1)}, bf16[2,160,2048]{2,1,0:T(8,128)(2,1)}, bf16[2,512,640]{2,1,0:T(8,128)(2,1)}, f32[2,160,2048]{2,1,0:T(8,12...) custom-call(f32[8,128]{1,0:T(8,128)} %get-tuple-element.39.total, ...), custom_call_target="tpu_custom_call" | custom-call | tf_op jit(solution)/shard_map/optimizer/pallas_call | solution.py:938

commit v3 on v0

v3 whole, which is shorter than its diff:
```python
import dataclasses
import functools

import jax
import jax.numpy as jnp
from jax import lax
from jax.experimental import pallas as pl
from jax.experimental.pallas import tpu as pltpu
from jax.sharding import PartitionSpec as P

BF, F32 = jnp.bfloat16, jnp.float32
LANES = 128
TILE = 1024
SMALL = 512
HALF = 256
ROWS = 512
CUT_TILE = 1024
VMEM_LIMIT = 67043328
NT = (((1,), (1,)), ((), ()))
NN = (((1,), (0,)), ((), ()))


@dataclasses.dataclass(frozen=True)
class Dims:
    layers: int
    tokens: int
    d: int
    ff: int
    n: int

    @property
    def own_ff(self):
        return self.ff // self.n

    @property
    def rows(self):
        return self.d // self.n

    @property
    def chunk(self):
        return self.n * LANES

    @property
    def chunks(self):
        return self.own_ff // LANES

    @property
    def tiles(self):
        return self.tokens // TILE

    @property
    def small(self):
        return self.tokens // SMALL

    @property
    def packed(self):
        return self.rows + self.d // 2 // self.n


def dot(a, b, dims=NN):
    return lax.dot_general(a, b, dims, preferred_element_type=F32)


def sliced(i, size):
    return pl.ds(pl.multiple_of(i * size, size), size)


def ring(n):
    me = lax.axis_index("dp")
    return me, lax.rem(me + 1, n), lax.rem(me + n - 1, n)


def partner():
    rep = lax.axis_index("rep")
    core = lax.rem(rep, 2)
    return core, rep + 1 - 2 * core


def greet(*others):
    for other in others:
        pl.semaphore_signal(pltpu.get_barrier_semaphore(), inc=1, device_id=other, device_id_type=pl.DeviceIdType.MESH)


def greeted(count):
    pl.semaphore_wait(pltpu.get_barrier_semaphore(), count)


def remote(src, dst, send, recv, device):
    return pltpu.make_async_remote_copy(src_ref=src, dst_ref=dst, send_sem=send, recv_sem=recv, device_id=device, device_id_type=pl.DeviceIdType.MESH)


def scale_of(wide, axis, count):
    return lax.rsqrt(jnp.sum(wide * wide, axis, keepdims=True) / count + 1e-6)


def move(src, dst, sem):
    return pltpu.make_async_copy(src, dst, sem)


class Gather:
    COPIES = 14

    def __init__(self, dm, w, sends, recvs):
        self.dm, self.w, self.sends, self.recvs = dm, w, sends, recvs
        self.me, self.right, self.left = ring(dm.n)
        self.far = lax.rem(self.me + 2, dm.n)
        self.core, self.other = partner()

    def slot(self, unit):
        return lax.rem(unit, self.w.shape[0])

    def _both(self, unit, source):
        half = self.dm.rows // 2
        at = pl.multiple_of(source * self.dm.rows + self.core * half, half)
        return self.w.at[self.slot(unit), 0:2, pl.ds(at, half), :]

    def _one(self, unit, which, source):
        half = self.dm.rows // 2
        at = pl.multiple_of(source * self.dm.rows + self.core * half, half)
        return self.w.at[self.slot(unit), which, pl.ds(at, half), :]

    def _down(self, unit, source, quarter=None):
        half = self.dm.d // 2
        columns = pl.ds(pl.multiple_of(source * LANES, LANES), LANES)
        if quarter is None:
            return self.w.at[self.slot(unit), 2, pl.ds(pl.multiple_of(self.core * half, half), half), columns]
        return self.w.at[self.slot(unit), 2, pl.ds(pl.multiple_of(self.core * half + quarter * (half // 2), half // 2), half // 2), columns]

    def _copy(self, unit, index, ref, device):
        return remote(ref, ref, self.sends.at[unit, index], self.recvs.at[unit, index], device)

    def own(self, unit, part):
        ref = self._down(unit, self.me) if part else self._both(unit, self.me)
        return [self._copy(unit, 2 * to + part, ref, device) for to, device in enumerate(({"dp": self.right}, {"dp": self.left}))]

    def relayed(self, unit, part):
        if part:
            right, left = self._down(unit, self.left, 0), self._down(unit, self.right, 1)
        else:
            right, left = self._one(unit, 0, self.left), self._one(unit, 1, self.right)
        return [self._copy(unit, 4 + part, right, {"dp": self.right}), self._copy(unit, 6 + part, left, {"dp": self.left})]

    def shared(self, unit, part, sources):
        out = []
        for s in sources:
            source = (self.left, self.right, self.far)[s]
            ref = self._down(unit, source) if part else self._both(unit, source)
            out.append(self._copy(unit, 8 + 2 * s + part, ref, {"rep": self.other}))
        return out

    def _arrivals(self, unit, index, ref):
        return remote(ref, ref, self.sends.at[unit, index], self.recvs.at[unit, index], {"dp": self.right})

    def step1(self, unit, parts=(0, 1)):
        for part in parts:
            for copy in self.own(unit, part):
                copy.start()

    def step2(self, unit):
        for part in range(2):
            for to, source in enumerate((self.left, self.right)):
                ref = self._down(unit, source) if part else self._both(unit, source)
                self._arrivals(unit, 2 * to + part, ref).wait_recv()
            for copy in self.relayed(unit, part) + self.shared(unit, part, (0, 1)):
                copy.start()

    def step3(self, unit):
        for part in range(2):
            for k in range(2):
                ref = self._down(unit, self.far, k) if part else self._one(unit, k, self.far)
                self._arrivals(unit, 4 + 2 * k + part, ref).wait_recv()
            for copy in self.shared(unit, part, (2,)):
                copy.start()

    def _theirs(self, unit, s):
        dm, other = self.dm, 1 - self.core
        source = (self.left, self.right, self.far)[s]
        half = dm.rows // 2
        at = pl.multiple_of(source * dm.rows + other * half, half)
        columns = pl.ds(pl.multiple_of(source * LANES, LANES), LANES)
        rows = pl.ds(pl.multiple_of(other * (dm.d // 2), dm.d // 2), dm.d // 2)
        return self.w.at[self.slot(unit), 0:2, pl.ds(at, half), :], self.w.at[self.slot(unit), 2, rows, columns]

    def done(self, unit):
        for s in range(3):
            both, down = self._theirs(unit, s)
            self._arrivals(unit, 8 + 2 * s, both).wait_recv()
            self._arrivals(unit, 9 + 2 * s, down).wait_recv()

    def drain(self, unit):
        for part in range(2):
            for copy in self.own(unit, part) + self.relayed(unit, part) + self.shared(unit, part, (0, 1, 2)):
                copy.wait_send()

    def fetch(self, unit, sources, sem):
        dm = self.dm
        layer, chunk = unit // dm.chunks, lax.rem(unit, dm.chunks)
        for which in range(2):
            for q in range(dm.n):
                columns = pl.ds(pl.multiple_of(q * dm.own_ff + chunk * LANES, LANES), LANES)
                to = self.w.at[self.slot(unit), which, sliced(self.me, dm.rows), q * LANES : (q + 1) * LANES]
                move(sources[which].at[layer, :, columns], to, sem.at[unit]).start()

    def fetched(self, unit, sem):
        ref = self.w.at[self.slot(unit), 0:2, sliced(self.me, self.dm.rows), :]
        move(ref, ref, sem.at[unit]).wait()

    def turn(self, unit, natural):
        columns = pl.ds(pl.multiple_of(self.me * LANES, LANES), LANES)
        self.w[self.slot(unit), 2, :, columns] = natural[sliced(lax.rem(unit, self.dm.chunks), LANES), :].T


class Scatter:
    def __init__(self, dm, wide, term, place, slots, send, recv, sends, recvs):
        self.dm, self.wide, self.term, self.place, self.slots = dm, wide, term, place, slots
        self.send, self.recv, self.sends, self.recvs = send, recv, sends, recvs
        self.me, self.right, self.left = ring(dm.n)
        self.far = lax.rem(self.me + 2, dm.n)

    def _copy(self, c, kind):
        device = {"dp": self.right if kind % 2 == 0 else self.left}
        slot = lax.rem(c, self.slots)
        return remote(self.place(self.send, c, kind), self.place(self.recv, c, kind), self.sends.at[slot, kind], self.recvs.at[slot, kind], device)

    def _parts(self, c, owner, half):
        dm = self.dm
        if self.wide:
            return [(self.term(c, half)[sliced(owner, dm.rows), :], slice(None))]
        columns = pl.ds(pl.multiple_of(owner * LANES, LANES), LANES)
        size = dm.d // 2 // dm.n
        own = self.term(c, half).at[:, columns]
        return [(own[pl.ds(half * (dm.d // 2) + i * size, size), :], slice(i * LANES, (i + 1) * LANES)) for i in range(dm.n)]

    def _put(self, c, kind, owner, half, add=None):
        to = self.place(self.send, c, kind)
        for term, columns in self._parts(c, owner, half):
            if add is not None:
                term = term + self.place(self.recv, c, add)[:, columns].astype(F32)
            to[:, columns] = term.astype(BF)
        self._copy(c, kind).start()

    def step1(self, c):
        self._put(c, 0, self.far, 0)
        self._put(c, 1, self.far, 1)
        self._put(c, 2, self.right, 1)
        self._put(c, 3, self.left, 0)

    def step2(self, c):
        for kind, owner, half in ((0, self.right, 0), (1, self.left, 1)):
            self._copy(c, kind).wait_recv()
            self._put(c, kind + 4, owner, half, add=kind)
        for kind in (0, 1):
            self._copy(c, kind).wait_send()

    def step3(self, c, put, squares):
        for kind in (2, 3, 4, 5):
            self._copy(c, kind).wait_recv()
        for half, kinds in ((0, (4, 3)), (1, (2, 5))):
            for term, columns in self._parts(c, self.me, half):
                for kind in kinds:
                    term = term + self.place(self.recv, c, kind)[:, columns].astype(F32)
                g = term.astype(BF)
                put(half, columns, g)
                g = g.astype(F32)
                g = jnp.sum((g * g).reshape(-1, 8, g.shape[-1]), 0)
                for j in range(0, g.shape[-1], LANES):
                    squares[...] += g[:, j : j + LANES]
        for kind in (2, 3, 4, 5):
            self._copy(c, kind).wait_send()


def back_through(gate, up, by_act):
    by_act = by_act.astype(BF).astype(F32)
    s = jax.nn.sigmoid(gate)
    by_up = (by_act * (gate * s)).astype(BF)
    by_gate = (by_act * up * (s * (1.0 + gate * (1.0 - s)))).astype(BF)
    return by_gate, by_up


def hidden_of(gate, up):
    return (gate * jax.nn.sigmoid(gate) * up).astype(BF)


def add_to(ref, first, term):
    ref[...] = jnp.where(first, 0.0, ref[...]) + term


def whole_kernel(
    dm, x, dy, w_gate, w_up, w_down,
    grads_out, total_out, gates, ups, acts, a0t, wd0, by_gates, by_ups,
    abuf, at, xt, dyb, dytb, big, w, natural, wsend, wrecv, dsend, drecv, squares, everyone,
    own_sem, nat_sem, x_sem, dy_sem, st_sem, by_sem, in_sem, gu_sem, ab_sem, misc_sem, g_sem, ready,
    gsends, grecvs, wsends, wrecvs, dsends, drecvs, ssends, srecvs,
):
    chunks, tiles, small, units = dm.chunks, dm.tiles, dm.small, dm.layers * dm.chunks
    steps = chunks * tiles
    gather = Gather(dm, w, gsends, grecvs)
    me, left, right, far = gather.me, gather.left, gather.right, gather.far
    sources = (w_gate, w_up)
    big_block = lambda i, width: big.at[:, pl.ds(pl.multiple_of(i * width, width), width)]
    saved = [move(w.at[c, 2], wd0.at[c], misc_sem.at[c]) for c in range(chunks - 1)]
    at_last = [move(wd0.at[c], w.at[chunks - 1, c], misc_sem.at[3 + c]) for c in range(chunks - 2)]
    at_end = move(wd0.at[chunks - 2], w.at[chunks, 0], misc_sem.at[5])
    a0t_out, a0t_back = move(at, a0t, misc_sem.at[6]), move(a0t, at, misc_sem.at[7])
    rest = dm.tokens // 2
    dy_back = move(dy.at[rest:, :], dyb.at[rest:, :], misc_sem.at[8])

    greet({"dp": right}, {"dp": left}, {"rep": gather.other}, {"dp": far})
    gather.fetch(0, sources, own_sem)
    move(w_down.at[0], natural, nat_sem.at[0]).start()
    for t in range(small):
        move(x.at[pl.ds(t * SMALL, SMALL), :], abuf.at[pl.ds(t * SMALL, SMALL), :], x_sem.at[t]).start()
    gather.fetched(0, own_sem)
    greeted(4)
    gather.step1(0, (0,))
    move(w_down.at[0], natural, nat_sem.at[0]).wait()
    gather.turn(0, natural)
    gather.step1(0, (1,))
    for u in range(1, chunks + 1):
        gather.fetch(u, sources, own_sem)
    for t in range(small):
        move(dy.at[pl.ds(t * SMALL, SMALL), :], dyb.at[pl.ds(t * SMALL, SMALL), :], dy_sem.at[t]).start()

    @pl.loop(0, 2 * small)
    def _(t):
        @pl.when(lax.rem(t, 2) == 0)
        def _():
            ref = abuf.at[sliced(t // 2, SMALL), :]
            move(ref, ref, x_sem.at[t // 2]).wait()

        at_t = sliced(t, HALF)
        tile = abuf[at_t, :]
        wide = tile.astype(F32)
        a = (wide * scale_of(wide, -1, dm.d)).astype(BF)
        xt[:, at_t] = tile.T
        at[:, at_t] = a.T
        abuf[at_t, :] = a

    gather.step2(0)

    @pl.loop(1, chunks)
    def _(u):
        gather.turn(u, natural)

    move(w_down.at[1], natural, nat_sem.at[1]).start()
    gather.fetched(1, own_sem)
    gather.step1(1)
    a0t_out.start()

    @pl.loop(0, small)
    def _(t):
        at_t = sliced(t, SMALL)
        move(dy.at[at_t, :], dyb.at[at_t, :], dy_sem.at[t]).wait()
        dytb[:, at_t] = dyb[at_t, :].T

    squares[...] = jnp.zeros_like(squares)
    move(w_down.at[1], natural, nat_sem.at[1]).wait()
    gather.turn(chunks, natural)
    gather.step3(0)

    def forward(gst, ust):
        def ast(slot):
            return dyb.at[pl.ds(pl.multiple_of(rest + slot * TILE, TILE), TILE), 0 : dm.chunk]

        def stored(i):
            slot, chunk, at_t = lax.rem(i, 2), i // tiles, sliced(lax.rem(i, tiles), TILE)
            pairs = ((gst.at[slot], gates), (ust.at[slot], ups), (ast(slot), acts))
            return [move(a, b.at[chunk, at_t, :], st_sem.at[k, slot]) for k, (a, b) in enumerate(pairs)]

        def tile_step(i, last):
            c, t = i // tiles, lax.rem(i, tiles)
            slot, at_t = lax.rem(i, 2), sliced(t, TILE)

            @pl.when(t == 0)
            def _():
                gather.done(c)

            if not last:
                for k in range(chunks - 1):

                    @pl.when(i == k * tiles)
                    def _():
                        saved[k].start()

                    @pl.when(i == k * tiles + 3)
                    def _():
                        saved[k].wait()

            @pl.when(t == 1)
            def _():
                gather.step2(c + 1)

            if not last:

                @pl.when(i == tiles + 1)
                def _():
                    gather.drain(0)
                    gather.fetch(chunks + 1, sources, own_sem)
                    gather.turn(chunks + 1, natural)

                @pl.when(t == 1)
                def _():
                    gather.fetched(c + 2, own_sem)
                    gather.step1(c + 2)

                @pl.when(i == 2 * tiles + 3)
                def _():
                    gather.drain(1)
                    gather.fetch(chunks + 2, sources, own_sem)
                    gather.turn(chunks + 2, natural)
                    gather.fetched(chunks + 1, own_sem)
                    gather.step1(chunks + 1)

            else:

                @pl.when(t == 1)
                def _():
                    gather.drain(2)
                    gather.fetch(chunks + 3, sources, own_sem)
                    gather.turn(chunks + 3, natural)

                @pl.when(t == 2)
                def _():
                    gather.step2(c + 2)

            @pl.when(t == 3)
            def _():
                gather.step3(c + 1)

            @pl.when(i >= 1)
            def _():
                for copy in stored(i - 1):
                    copy.start()

            @pl.when(i >= 2)
            def _():
                for copy in stored(i - 2):
                    copy.wait()

            hidden = ast(slot)
            for r in range(0, TILE, SMALL):
                a, rows = abuf[sliced(t * (TILE // SMALL) + r // SMALL, SMALL), :], slice(r, r + SMALL)
                for b in range(0, dm.chunk, HALF):
                    part = slice(b, b + HALF)
                    gate = dot(a, w[c, 0, :, part])
                    up = dot(a, w[c, 1, :, part])
                    gst[slot, rows, part] = gate
                    ust[slot, rows, part] = up
                    hidden[rows, part] = hidden_of(gate, up)
            if not last:
                add_to(big.at[:, at_t], c == 0, dot(w[c, 2], hidden[...], NT))
                return
            for b in range(0, TILE, HALF):
                at_b = pl.ds(pl.multiple_of(t * TILE + b, HALF), HALF)
                total = big[:, at_b] + dot(w[c, 2], hidden[b : b + HALF, :], NT)
                h = xt[:, at_b] + total.astype(BF)
                wide = h.astype(F32)
                a = (wide * scale_of(wide, 0, dm.d)).astype(BF)
                xt[:, at_b] = h
                at[:, at_b] = a
                abuf[at_b, :] = a.T

        @pl.loop(0, steps - tiles)
        def _(i):
            tile_step(i, False)

        a0t_out.wait()

        @pl.loop(steps - tiles, steps)
        def _(i):
            tile_step(i, True)

        for copy in stored(steps - 1):
            copy.start()
        gather.step3(chunks + 1)
        gather.fetched(chunks + 2, own_sem)
        gather.step1(chunks + 2)
        gather.drain(chunks - 1)
        for copy in at_last:
            copy.start()
        for i in range(steps - 2, steps):
            for copy in stored(i):
                copy.wait()

    pl.run_scoped(forward, pltpu.VMEM((2, TILE, dm.chunk), F32), pltpu.VMEM((2, TILE, dm.chunk), F32))

    def full(buffer, c, kind):
        return buffer.at[lax.rem(c, buffer.shape[0]), kind]

    def pair(buffer, c, kind):
        return buffer.at[lax.rem(c, 2), kind]

    def cut(buffer, c, kind):
        slot = lax.rem(c, 4)
        return buffer.at[slot // 2, kind, :, pl.ds(pl.multiple_of(lax.rem(slot, 2) * HALF, HALF), HALF)]

    def backward1(ba, bg, bu, stash, grads):
        wides = Scatter(
            dm, True, lambda c, half: big_block(2 * lax.rem(c, 2) + half, dm.chunk), pair, 2, wsend, wrecv, wsends, wrecvs
        )
        downs = Scatter(dm, False, lambda c, half: big_block(4 + lax.rem(c, 2), dm.chunk), pair, 2, dsend, drecv, dsends, drecvs)

        def stored(i):
            slot, chunk, at_t = lax.rem(i, 2), i // tiles, sliced(lax.rem(i, tiles), TILE)
            return [move(a.at[slot], b.at[chunk, at_t, :], by_sem.at[k, slot]) for k, (a, b) in enumerate(((bg, by_gates), (bu, by_ups)))]

        def step1(c):
            wides.step1(c)
            downs.step1(c)

        def step2(c):
            wides.step2(c)
            downs.step2(c)

        out = lambda c: move(grads.at[lax.rem(c, 2)], grads_out.at[1, c], g_sem.at[1 + lax.rem(c, 2)])

        def step3(c, again):
            if again is True:
                out(c - 2).wait()

            def put(first, last):
                def put(half, columns, g):
                    grads[lax.rem(c, 2), half * dm.packed + first : half * dm.packed + last, columns] = g

                return put

            wides.step3(c, put(0, dm.rows), squares)
            downs.step3(c, put(dm.rows, dm.packed), squares)
            out(c).start()

        def gate_tile(slot, c):
            return at.at[0:SMALL, pl.ds(pl.multiple_of((slot * chunks + c) * dm.chunk, dm.chunk), dm.chunk)]

        def up_tile(slot, c):
            return dyb.at[sliced(slot * chunks + c, SMALL), 0 : dm.chunk]

        def inputs(t):
            slot, at_t = lax.rem(t, 2), sliced(t, SMALL)
            return [
                move(src.at[c, at_t, :], tile(slot, c), in_sem.at[k, slot, c])
                for k, (src, tile) in enumerate(((by_gates, gate_tile), (by_ups, up_tile)))
                for c in range(chunks)
            ]

        @pl.loop(0, steps)
        def _(i):
            c, t = i // tiles, lax.rem(i, tiles)
            slot, at_t = lax.rem(i, 2), sliced(t, TILE)

            @pl.when(t == 0)
            def _():
                gather.done(chunks + c)

            @pl.when(i == 0)
            def _():
                dy_back.start()

            @pl.when(i == 2)
            def _():
                dy_back.wait()

            @pl.when(jnp.logical_and(t == 0, c >= 2))
            def _():
                step3(c - 2, False)

            @pl.when(jnp.logical_and(t == 0, c >= 1))
            def _():
                step1(c - 1)

            @pl.when(i == 2)
            def _():
                gather.step2(units - 2)
                gather.fetched(units - 1, own_sem)
                gather.step1(units - 1)

            @pl.when(i == 3)
            def _():
                gather.step3(units - 2)

            @pl.when(i == 5)
            def _():
                gather.step2(units - 1)

            @pl.when(i == 7)
            def _():
                gather.step3(units - 1)

            @pl.when(jnp.logical_and(t == 2, c >= 1))
            def _():
                step2(c - 1)

            @pl.when(i >= 1)
            def _():
                for copy in stored(i - 1):
                    copy.start()

            @pl.when(i >= 2)
            def _():
                for copy in stored(i - 2):
                    copy.wait()

            @pl.when(i == steps - 1)
            def _():
                for copy in inputs(0):
                    copy.start()

            s = gather.slot(chunks + c)
            for r in range(0, TILE, ROWS):
                tokens, rows = sliced(t * (TILE // ROWS) + r // ROWS, ROWS), slice(r, r + ROWS)
                a, y = abuf[tokens, :], dyb[tokens, :]
                for b in range(0, dm.chunk, HALF):
                    part = slice(b, b + HALF)
                    gate, up = dot(a, w[s, 0, :, part]), dot(a, w[s, 1, :, part])
                    by_gate, by_up = back_through(gate, up, dot(y, w[s, 2, :, part]))
                    ba[rows, part] = hidden_of(gate, up)
                    bg[slot, rows, part] = by_gate
                    bu[slot, rows, part] = by_up
            add_to(wides.term(c, 0), t == 0, dot(at[:, at_t], bg[slot]))
            add_to(wides.term(c, 1), t == 0, dot(at[:, at_t], bu[slot]))
            add_to(downs.term(c, 0), t == 0, dot(dytb[:, at_t], ba[...]))

        last = chunks - 1
        for copy in stored(steps - 1):
            copy.start()
        step3(last - 1, True)
        step1(last)
        for i in range(steps - 2, steps):
            for copy in stored(i):
                copy.wait()

        def matmuls(t):
            slot, total = lax.rem(t, 2), None
            for c in range(chunks):
                s = (chunks + c) % (chunks + 1)
                term = dot(w[s, 0], gate_tile(slot, c)[...], NT) + dot(w[s, 1], up_tile(slot, c)[...], NT)
                total = term if total is None else total + term
            return total.astype(BF)

        def finish(t):
            for k in range(0, SMALL, LANES):
                at_k = sliced(t * (SMALL // LANES) + k // LANES, LANES)
                by_a = stash[:, k : k + LANES].astype(F32)
                h = xt[:, at_k].astype(F32)
                square = jnp.sum(h * h, 0, keepdims=True) / dm.d + 1e-6
                scale = lax.rsqrt(square)
                along = jnp.sum(h * by_a, 0, keepdims=True) * (scale / square) / dm.d
                by_h = dytb[:, at_k] + (by_a * scale - h * along).astype(BF)
                dytb[:, at_k] = by_h
                abuf[at_k, :] = by_h.T

        for copy in inputs(1):
            copy.start()
        for copy in inputs(0):
            copy.wait()
        stash[...] = matmuls(0)

        @pl.loop(1, small)
        def _(t):
            @pl.when(t == 3)
            def _():
                step2(last)

            @pl.when(t == 6)
            def _():
                step3(last, True)
                for neighbour in (left, right):
                    pl.semaphore_signal(ready, inc=1, device_id={"dp": neighbour}, device_id_type=pl.DeviceIdType.MESH)

            for copy in inputs(t):
                copy.wait()

            @pl.when(t + 1 < small)
            def _():
                for copy in inputs(t + 1):
                    copy.start()

            @pl.when(t == small - 1)
            def _():
                hidden(0).start()

            finish(t - 1)
            stash[...] = matmuls(t)

        hidden(1).start()
        a0t_back.start()
        for u in range(chunks, units):
            gather.drain(u)
        at_end.start()
        finish(small - 1)
        for c in (last - 1, last):
            out(c).wait()

    span = dm.tokens // 2

    def hidden_at(i):
        return dyb.at[sliced(lax.rem(i, 2), span), 0 : dm.chunk]

    def hidden(i):
        return move(acts.at[i // 2, sliced(lax.rem(i, 2), span), :], hidden_at(i), ab_sem.at[lax.rem(i, 2)])

    pl.run_scoped(
        backward1,
        pltpu.VMEM((TILE, dm.chunk), BF), pltpu.VMEM((2, TILE, dm.chunk), BF), pltpu.VMEM((2, TILE, dm.chunk), BF), pltpu.VMEM((dm.d, SMALL), BF),
        pltpu.VMEM((2, 2 * dm.packed, dm.chunk), BF),
    )

    def backward0(gb, ub, bg, bu):
        cuts, parts = dm.chunk // HALF, dm.tokens // gb.shape[1]
        wides = Scatter(
            dm, True, lambda u, half: big_block(2 * chunks * cuts // 2 + 2 * lax.rem(u, 4) + half, HALF), cut, 4, wsend, wrecv, wsends, wrecvs
        )
        downs = Scatter(dm, False, lambda c, half: big_block(c, dm.chunk), full, chunks, dsend, drecv, dsends, drecvs)

        def inputs(i):
            slot, unit, at_t = lax.rem(i, 2), i // parts, sliced(lax.rem(i, parts), gb.shape[1])
            columns = pl.ds(pl.multiple_of(lax.rem(unit, cuts) * HALF, HALF), HALF)
            return (
                move(gates.at[unit // cuts, at_t, columns], gb.at[slot], gu_sem.at[0, slot]),
                move(ups.at[unit // cuts, at_t, columns], ub.at[slot], gu_sem.at[1, slot]),
            )

        @pl.loop(0, 2 * chunks)
        def _(i):
            c, t = i // 2, lax.rem(i, 2)

            @pl.when(i == 1)
            def _():
                pl.semaphore_wait(ready, 2)

            @pl.when(jnp.logical_and(i >= 1, i + 1 < 2 * chunks))
            def _():
                hidden(i + 1).start()

            @pl.when(i == 5)
            def _():
                for copy in (*inputs(0), *inputs(1)):
                    copy.start()

            hidden(i).wait()
            add_to(downs.term(c, 0), t == 0, dot(dytb[:, sliced(t, span)], hidden_at(i)[...]))

            @pl.when(t == 1)
            def _():
                downs.step1(c)

        a0t_back.wait()
        at_end.wait()
        for copy in at_last:
            copy.wait()

        def sums(c):
            return w.at[c // 3, lax.rem(c, 3), 0 : 2 * dm.packed, :]

        def put_down(c):
            def put(half, columns, g):
                sums(c)[pl.ds(half * dm.packed + dm.rows, dm.packed - dm.rows), columns] = g

            return put

        def put_wide(unit):
            def put(half, columns, g):
                to = sums(unit // cuts).at[:, pl.ds(pl.multiple_of(lax.rem(unit, cuts) * HALF, HALF), HALF)]
                to[pl.ds(half * dm.packed, dm.rows), :] = g

            return put

        cut_units = chunks * cuts
        first, middle = 0, parts // 2

        @pl.loop(0, cut_units * parts)
        def _(i):
            unit, t, slot = i // parts, lax.rem(i, parts), lax.rem(i, 2)

            @pl.when(jnp.logical_and(t == first, unit >= 1))
            def _():
                wides.step1(unit - 1)

            @pl.when(jnp.logical_and(t == middle, unit >= 3))
            def _():
                wides.step3(unit - 3, put_wide(unit - 3), squares)

            @pl.when(jnp.logical_and(t == middle, unit >= 2))
            def _():
                wides.step2(unit - 2)

            @pl.when(i < chunks)
            def _():
                downs.step2(i)

            @pl.when(jnp.logical_and(i >= 2 * chunks, i < 3 * chunks))
            def _():
                downs.step3(i - 2 * chunks, put_down(i - 2 * chunks), squares)

            @pl.when(jnp.logical_and(i >= 1, i + 1 < cut_units * parts))
            def _():
                for copy in inputs(i + 1):
                    copy.start()

            for copy in inputs(i):
                copy.wait()
            c = unit // cuts
            slot_w, which = chunks - 1 + (c // 2) * (1 - lax.rem(c, 2)), lax.rem(c, 2) * (1 + c // 2)
            weights = w[slot_w, which, :, pl.ds(pl.multiple_of(lax.rem(unit, cuts) * HALF, HALF), HALF)]
            size = gb.shape[1]
            blocks = [(slice(b, b + SMALL), sliced(t * (size // SMALL) + b // SMALL, SMALL)) for b in range(0, size, SMALL)]
            by_acts = [dot(abuf[tokens, :], weights) for _, tokens in blocks]
            totals = [None, None]
            for (rows, tokens), by_act in zip(blocks, by_acts, strict=True):
                bg[rows, :], bu[rows, :] = back_through(gb[slot, rows, :], ub[slot, rows, :], by_act)
                for k, right in enumerate((bg, bu)):
                    term = dot(at[:, tokens], right[rows, :])
                    totals[k] = term if totals[k] is None else totals[k] + term
            for k in range(2):
                add_to(wides.term(unit, k), t == 0, totals[k])

        last = cut_units - 1
        wides.step1(last)
        wides.step2(last - 1)
        wides.step3(last - 2, put_wide(last - 2), squares)
        wides.step2(last)
        wides.step3(last - 1, put_wide(last - 1), squares)
        wides.step3(last, put_wide(last), squares)
        out = [move(sums(c), grads_out.at[0, c], g_sem.at[1 + c]) for c in range(chunks)]
        for copy in out:
            copy.start()
        copies = []
        for k in range(1, dm.n):
            to = lax.rem(me + k, dm.n)
            copies.append(remote(squares, everyone.at[me], ssends.at[k - 1], srecvs.at[k - 1], {"dp": to}))
        for copy in copies:
            copy.start()
        everyone[me] = squares[...]
        for copy in copies:
            copy.wait()
        total = everyone[0]
        for k in range(1, dm.n):
            total = total + everyone[k]
        total_out[...] = total
        for copy in out:
            copy.wait()

    part = CUT_TILE
    pl.run_scoped(
        backward0,
        pltpu.VMEM((2, part, HALF), F32), pltpu.VMEM((2, part, HALF), F32), pltpu.VMEM((part, HALF), BF), pltpu.VMEM((part, HALF), BF),
    )


def optimizer_kernel(dm, total, grads_in, *refs):
    ins, outs, (grads, *buffers), (g_sem, in_sem, out_sem) = refs[:9], refs[9:18], refs[18:25], refs[25:]
    stores = [buffers[0:2], buffers[2:4], buffers[4:6]]
    halves = 2
    pieces = [(layer, which, half) for layer in range(dm.layers) for which in range(3) for half in range(halves)]

    def places(piece):
        layer, which, half = piece
        out = []
        for kind in range(3):
            if which < 2:
                cut = slice(half * dm.ff // halves, (half + 1) * dm.ff // halves)
                here = stores[kind][0].at[2 * layer + which, :, cut]
                out.append((ins[3 * kind + which].at[layer, :, cut], here, outs[3 * kind + which].at[layer, :, cut]))
            else:
                cut = slice(half * dm.own_ff // halves, (half + 1) * dm.own_ff // halves)
                here = stores[kind][1].at[layer, cut, :]
                out.append((ins[3 * kind + which].at[layer, cut, :], here, outs[3 * kind + which].at[layer, cut, :]))
        return out

    fetch = [move(grads_in.at[layer], grads.at[layer], g_sem.at[layer]) for layer in range(dm.layers)]
    loads = [[move(a, b, in_sem.at[k, kind]) for kind, (a, b, _) in enumerate(places(p))] for k, p in enumerate(pieces)]
    writes = [[move(b, c, out_sem.at[k, kind]) for kind, (_, b, c) in enumerate(places(p))] for k, p in enumerate(pieces)]
    for layer in range(dm.layers):
        fetch[layer].start()
        for k, piece in enumerate(pieces):
            if piece[0] == layer:
                for copy in loads[k]:
                    copy.start()
    count = dm.layers * 3 * dm.d * dm.ff
    factor = jnp.minimum(1.0, 0.5 * lax.rsqrt(jnp.sum(total[...]) / count + 1e-30))
    size = dm.d // 2 // dm.n

    def adamw(g, refs, at):
        w, m, v = (ref[at] for ref in refs)
        g = g.astype(F32) * factor
        w = w.astype(F32)
        m = 0.9 * m + 0.1 * g
        v = 0.95 * v + 0.05 * g * g
        change = m * lax.rsqrt(v + 1e-8) + 0.1 * w
        refs[0][at] = (w - 0.02 * change).astype(BF)
        refs[1][at] = m
        refs[2][at] = v

    for k, (layer, which, half) in enumerate(pieces):
        if (which, half) == (0, 0):
            fetch[layer].wait()
        for copy in loads[k]:
            copy.wait()
        refs = [here for _, here, _ in places(pieces[k])]
        if which < 2:
            for b in range(dm.ff // halves // LANES):
                q, c = divmod(half * dm.ff // halves // LANES + b, dm.chunks)
                g = grads[layer, c, which * dm.packed : which * dm.packed + dm.rows, q * LANES : (q + 1) * LANES]
                adamw(g, refs, (slice(None), slice(b * LANES, (b + 1) * LANES)))
        else:
            for b in range(dm.own_ff // halves // LANES):
                c = half * dm.own_ff // halves // LANES + b
                for row in range(2 * dm.n):
                    side, i = divmod(row, dm.n)
                    start = side * dm.packed + dm.rows
                    g = grads[layer, c, start : start + size, i * LANES : (i + 1) * LANES]
                    if row == 0:
                        rows = []
                    rows.append(g)
                adamw(jnp.concatenate(rows, axis=0).T, refs, (slice(b * LANES, (b + 1) * LANES), slice(None)))
        for copy in writes[k]:
            copy.start()
    for copies in writes:
        for copy in copies:
            copy.wait()


def step(mesh, x, dy, *arrays):
    weights, m, v = (arrays[i : i + 3] for i in (0, 3, 6))
    x, dy = x[0], dy[0]
    w_gate, w_up, w_down = weights
    n = mesh.shape["dp"]
    dm = Dims(w_gate.shape[0], x.shape[0], x.shape[1], w_gate.shape[2], n)
    tokens, d, chunk, chunks, tiles = dm.tokens, dm.d, dm.chunk, dm.chunks, dm.tiles
    hbm = pl.BlockSpec(memory_space=pltpu.HBM)
    vmem = pl.BlockSpec(memory_space=pltpu.VMEM)
    shape = jax.ShapeDtypeStruct
    dma = lambda *s: pltpu.SemaphoreType.DMA(s)
    natural, turned, per_chunk = (tokens, d), (d, tokens), (chunks, tokens, chunk)
    block, wide, down = (2 * dm.packed, chunk), (dm.rows, chunk), (dm.packed - dm.rows, chunk)
    units = dm.layers * chunks
    semaphores = [
        dma(units), dma(2), dma(dm.small), dma(dm.small), dma(3, 2), dma(2, 2), dma(2, 2, chunks), dma(2, 2), dma(2), dma(9), dma(1 + chunks),
        pltpu.SemaphoreType.REGULAR,
        dma(units, Gather.COPIES), dma(units, Gather.COPIES), dma(4, 6), dma(4, 6), dma(chunks, 6), dma(chunks, 6), dma(n - 1), dma(n - 1),
    ]

    def kernel(*refs):
        pl.run_scoped(lambda *scoped: whole_kernel(dm, *refs, *scoped), *semaphores)

    grads, total, *_ = pl.pallas_call(
        kernel,
        out_shape=[
            shape((2, chunks, *block), BF), shape((8, LANES), F32), shape(per_chunk, F32), shape(per_chunk, F32), shape(per_chunk, BF),
            shape(turned, BF), shape((chunks - 1, d, chunk), BF), shape(per_chunk, BF), shape(per_chunk, BF),
        ],
        in_specs=[hbm] * 5,
        out_specs=[hbm, vmem] + [hbm] * 7,
        scratch_shapes=[
            pltpu.VMEM(natural, BF), pltpu.VMEM(turned, BF), pltpu.VMEM(turned, BF), pltpu.VMEM(natural, BF), pltpu.VMEM(turned, BF),
            pltpu.VMEM(turned, F32), pltpu.VMEM((chunks + 1, 3, d, chunk), BF), pltpu.VMEM((dm.own_ff, d), BF),
            pltpu.VMEM((2, 6, *wide), BF), pltpu.VMEM((2, 6, *wide), BF), pltpu.VMEM((chunks, 6, *down), BF), pltpu.VMEM((chunks, 6, *down), BF),
            pltpu.VMEM((8, LANES), F32), pltpu.VMEM((n, 8, LANES), F32),
        ],
        compiler_params=pltpu.CompilerParams(vmem_limit_bytes=VMEM_LIMIT, collective_id=0, has_side_effects=True),
        name="whole",
    )(x, dy, w_gate, w_up, w_down)

    wides, downs = (2 * dm.layers, dm.rows, dm.ff), (dm.layers, dm.own_ff, d)
    return tuple(
        pl.pallas_call(
            functools.partial(optimizer_kernel, dm),
            out_shape=[shape(w.shape, BF) for w in weights] + [shape(w.shape, F32) for w in weights] * 2,
            in_specs=[vmem] + [hbm] * 10,
            out_specs=[hbm] * 9,
            scratch_shapes=[
                pltpu.VMEM((2, chunks, *block), BF), pltpu.VMEM(wides, BF), pltpu.VMEM(downs, BF),
                pltpu.VMEM(wides, F32), pltpu.VMEM(downs, F32), pltpu.VMEM(wides, F32), pltpu.VMEM(downs, F32),
                dma(dm.layers), dma(6 * dm.layers, 3), dma(6 * dm.layers, 3),
            ],
            compiler_params=pltpu.CompilerParams(vmem_limit_bytes=VMEM_LIMIT),
            name="optimizer",
        )(total, grads, *weights, *m, *v)
    )


def solution(mesh):
    states, cut = P(("rep", "dp"), None, None), P(None, "dp", None)
    return jax.shard_map(
        functools.partial(step, mesh),
        mesh=mesh,
        in_specs=(states, states) + (cut,) * 9,
        out_specs=(P("rep", "dp", None),) * 9,
        check_vma=False,
    )
```

time: 569 us -> 280 us (0.49); the launches traced: 562 us -> 280 us
  matrix products: 366 us -> 0 us
  Pallas kernels: 0 us -> 279 us
  waiting for transfers between devices: 107 us -> 0 us
  other arithmetic: 35.8 us -> 0 us
  local copies, waits for them, and re-layouts: 25.3 us -> 0 us
  between operations: 17.6 us -> 0.82 us
  blocking collectives: 9.43 us -> 0 us
    dot_general x15 -> x0, matrix products: 366 us -> none  [the longest x5 136 us: layer(): gate = jnp.dot(a, w['w_gate'], preferred_element_type=jnp.float32)]
    pallas_call x0 -> x2, Pallas kernels: none -> 279 us  [the longest x1 263 us: step(): pl.pallas_call(kernel, out_shape=[shape((2, chunks, *block), BF), shape((...]
    all_gather x6 -> x0, waiting for transfers between devices: 57.3 us -> none  [fetched(): lax.all_gather(w[number], 'dp', axis=0, tiled=True)]
    reduce_scatter x6 -> x0, waiting for transfers between devices: 47.1 us -> none  [step(): lax.psum_scatter(by_w[name], 'dp', scatter_dimension=0, tiled=True)]
    unnamed x42 -> x0, local copies, waits for them, and re-layouts: 19.1 us -> none
    convert_element_type x2 -> x0, other arithmetic: 12.4 us -> none  [adamw(): return ((w - 0.02 * step).astype(jnp.bfloat16), m, v)]
    add_any x1 -> x0, other arithmetic: 11.9 us -> none  [normed(): wide = h.astype(jnp.float32)]
    reduce_sum x4 -> x0, other arithmetic: 11.5 us -> none  [the longest x3 7.88 us: step(): squares = lax.psum(sum((jnp.sum(g * g) for g in gradients)), 'dp')]
  transfers between devices with their start and end apart: 12 -> 0, of which waited for: 7 -> 0; matrix products, arithmetic and copies ran while one was open for 51% -> 0% of each run, Pallas kernels for 0% -> 0%
where the time goes in v3:
time: 280 us
  Pallas kernels  279 us (100%)
    pallas_call x1, Pallas kernels, step(): pl.pallas_call(kernel, out_shape=[shape((2, chunks, *block), BF), shape((...  263 us
    pallas_call x1, Pallas kernels, step(): pl.pallas_call(functools.partial(optimizer_kernel, dm), out_shape=[shape(...  15.5 us

profile of v3, /device:TPU:112, one launch (start us, length us, event | category | flops | bytes accessed | tf_op | source)
XLA Modules:
  0.0 279.8 jit_solution(5955452702639102772)
XLA Ops:
  0.6 263.4 %whole.1 = (bf16[2,4,480,512]{3,2,1,0:T(8,128)(2,1)}, f32[8,128]{1,0:T(8,128)}, f32[4,4096,512]{2,1,0:T(8,128)}, f32[4,4096,512]{2,1,0:T(8,128)}, bf16[4,4096,51...) custom-call(bf16[4096,640]{1,0:T(8,128)(2,1)} %bitcast.2, ...), custom_call_target="tpu_custom_call" | custom-call | tf_op jit(solution)/shard_map/whole/pallas_call | solution.py:945
  264.1 15.5 %optimizer.1 = (bf16[2,160,2048]{2,1,0:T(8,128)(2,1)}, bf16[2,160,2048]{2,1,0:T(8,128)(2,1)}, bf16[2,512,640]{2,1,0:T(8,128)(2,1)}, f32[2,160,2048]{2,1,0:T(8,12...) custom-call(f32[8,128]{1,0:T(8,128)} %get-tuple-element.11.total, ...), custom_call_target="tpu_custom_call" | custom-call | tf_op jit(solution)/shard_map/optimizer/pallas_call | solution.py:965

commit v4 on v3

--- a/solution.py
+++ b/solution.py
@@ -13,8 +13,9 @@
 TILE = 1024
 SMALL = 512
 HALF = 256
-ROWS = 512
-CUT_TILE = 1024
+ROWS = 1024
+PIECE = 512
+CUT_TILE = 2048
 VMEM_LIMIT = 67043328
 NT = (((1,), (1,)), ((), ()))
 NN = (((1,), (0,)), ((), ()))
@@ -239,11 +240,9 @@
             to[:, columns] = term.astype(BF)
         self._copy(c, kind).start()
 
-    def step1(self, c):
-        self._put(c, 0, self.far, 0)
-        self._put(c, 1, self.far, 1)
-        self._put(c, 2, self.right, 1)
-        self._put(c, 3, self.left, 0)
+    def step1(self, c, kinds=(0, 1, 2, 3)):
+        for kind in kinds:
+            self._put(c, kind, (self.far, self.far, self.right, self.left)[kind], (0, 1, 1, 0)[kind])
 
     def step2(self, c):
         for kind, owner, half in ((0, self.right, 0), (1, self.left, 1)):
@@ -287,8 +286,8 @@
 
 def whole_kernel(
     dm, x, dy, w_gate, w_up, w_down,
-    grads_out, total_out, gates, ups, acts, a0t, wd0, by_gates, by_ups,
-    abuf, at, xt, dyb, dytb, big, w, natural, wsend, wrecv, dsend, drecv, squares, everyone,
+    grads_out, squares_out, gates, ups, acts, a0t, wd0, by_gates, by_ups,
+    abuf, at, xt, dyb, dytb, big, w, natural, wsend, wrecv, dsend, drecv, squares,
     own_sem, nat_sem, x_sem, dy_sem, st_sem, by_sem, in_sem, gu_sem, ab_sem, misc_sem, g_sem, ready,
     gsends, grecvs, wsends, wrecvs, dsends, drecvs, ssends, srecvs,
 ):
@@ -419,7 +418,7 @@
                     gather.fetch(chunks + 3, sources, own_sem)
                     gather.turn(chunks + 3, natural)
 
-                @pl.when(t == 2)
+                @pl.when(t == 3)
                 def _():
                     gather.step2(c + 2)
 
@@ -472,7 +471,6 @@
 
         for copy in stored(steps - 1):
             copy.start()
-        gather.step3(chunks + 1)
         gather.fetched(chunks + 2, own_sem)
         gather.step1(chunks + 2)
         gather.drain(chunks - 1)
@@ -484,8 +482,9 @@
 
     pl.run_scoped(forward, pltpu.VMEM((2, TILE, dm.chunk), F32), pltpu.VMEM((2, TILE, dm.chunk), F32))
 
-    def full(buffer, c, kind):
-        return buffer.at[lax.rem(c, buffer.shape[0]), kind]
+    def spread(buffer, c, kind):
+        size = dm.packed - dm.rows
+        return buffer.at[kind * size : (kind + 1) * size, pl.ds(pl.multiple_of(c * dm.chunk, dm.chunk), dm.chunk)]
 
     def pair(buffer, c, kind):
         return buffer.at[lax.rem(c, 2), kind]
@@ -505,22 +504,24 @@
             return [move(a.at[slot], b.at[chunk, at_t, :], by_sem.at[k, slot]) for k, (a, b) in enumerate(((bg, by_gates), (bu, by_ups)))]
 
         def step1(c):
-            wides.step1(c)
-            downs.step1(c)
+            for kinds in ((0, 1), (2, 3)):
+                wides.step1(c, kinds)
+                downs.step1(c, kinds)
 
         def step2(c):
             wides.step2(c)
             downs.step2(c)
 
-        out = lambda c: move(grads.at[lax.rem(c, 2)], grads_out.at[1, c], g_sem.at[1 + lax.rem(c, 2)])
-
-        def step3(c, again):
-            if again is True:
-                out(c - 2).wait()
+        out = lambda c: move(grads, grads_out.at[1, c], g_sem.at[1])
+
+        def step3(c):
+            @pl.when(c >= 1)
+            def _():
+                out(c - 1).wait()
 
             def put(first, last):
                 def put(half, columns, g):
-                    grads[lax.rem(c, 2), half * dm.packed + first : half * dm.packed + last, columns] = g
+                    grads[half * dm.packed + first : half * dm.packed + last, columns] = g
 
                 return put
 
@@ -555,13 +556,17 @@
             def _():
                 dy_back.start()
 
+            @pl.when(i == 1)
+            def _():
+                gather.step3(chunks + 1)
+
             @pl.when(i == 2)
             def _():
                 dy_back.wait()
 
             @pl.when(jnp.logical_and(t == 0, c >= 2))
             def _():
-                step3(c - 2, False)
+                step3(c - 2)
 
             @pl.when(jnp.logical_and(t == 0, c >= 1))
             def _():
@@ -622,7 +627,7 @@
         last = chunks - 1
         for copy in stored(steps - 1):
             copy.start()
-        step3(last - 1, True)
+        step3(last - 1)
         step1(last)
         for i in range(steps - 2, steps):
             for copy in stored(i):
@@ -637,9 +642,9 @@
             return total.astype(BF)
 
         def finish(t):
-            for k in range(0, SMALL, LANES):
-                at_k = sliced(t * (SMALL // LANES) + k // LANES, LANES)
-                by_a = stash[:, k : k + LANES].astype(F32)
+            for k in range(0, SMALL, PIECE):
+                at_k = sliced(t * (SMALL // PIECE) + k // PIECE, PIECE)
+                by_a = stash[:, k : k + PIECE].astype(F32)
                 h = xt[:, at_k].astype(F32)
                 square = jnp.sum(h * h, 0, keepdims=True) / dm.d + 1e-6
                 scale = lax.rsqrt(square)
@@ -662,9 +667,7 @@
 
             @pl.when(t == 6)
             def _():
-                step3(last, True)
-                for neighbour in (left, right):
-                    pl.semaphore_signal(ready, inc=1, device_id={"dp": neighbour}, device_id_type=pl.DeviceIdType.MESH)
+                step3(last)
 
             for copy in inputs(t):
                 copy.wait()
@@ -686,9 +689,12 @@
         for u in range(chunks, units):
             gather.drain(u)
         at_end.start()
+        hidden(0).wait()
+        big[:, 0 : dm.chunk] = dot(dytb[:, 0:span], hidden_at(0)[...])
         finish(small - 1)
-        for c in (last - 1, last):
-            out(c).wait()
+        for neighbour in (left, right):
+            pl.semaphore_signal(ready, inc=1, device_id={"dp": neighbour}, device_id_type=pl.DeviceIdType.MESH)
+        out(last).wait()
 
     span = dm.tokens // 2
 
@@ -701,7 +707,7 @@
     pl.run_scoped(
         backward1,
         pltpu.VMEM((TILE, dm.chunk), BF), pltpu.VMEM((2, TILE, dm.chunk), BF), pltpu.VMEM((2, TILE, dm.chunk), BF), pltpu.VMEM((dm.d, SMALL), BF),
-        pltpu.VMEM((2, 2 * dm.packed, dm.chunk), BF),
+        pltpu.VMEM((2 * dm.packed, dm.chunk), BF),
     )
 
     def backward0(gb, ub, bg, bu):
@@ -709,7 +715,9 @@
         wides = Scatter(
             dm, True, lambda u, half: big_block(2 * chunks * cuts // 2 + 2 * lax.rem(u, 4) + half, HALF), cut, 4, wsend, wrecv, wsends, wrecvs
         )
-        downs = Scatter(dm, False, lambda c, half: big_block(c, dm.chunk), full, chunks, dsend, drecv, dsends, drecvs)
+        downs = Scatter(
+            dm, False, lambda c, half: big_block(c, dm.chunk), spread, chunks, xt.at[:, 0:rest], xt.at[:, rest:], dsends, drecvs
+        )
 
         def inputs(i):
             slot, unit, at_t = lax.rem(i, 2), i // parts, sliced(lax.rem(i, parts), gb.shape[1])
@@ -719,7 +727,7 @@
                 move(ups.at[unit // cuts, at_t, columns], ub.at[slot], gu_sem.at[1, slot]),
             )
 
-        @pl.loop(0, 2 * chunks)
+        @pl.loop(1, 2 * chunks)
         def _(i):
             c, t = i // 2, lax.rem(i, 2)
 
@@ -727,14 +735,16 @@
             def _():
                 pl.semaphore_wait(ready, 2)
 
-            @pl.when(jnp.logical_and(i >= 1, i + 1 < 2 * chunks))
+            @pl.when(i + 1 < 2 * chunks)
             def _():
                 hidden(i + 1).start()
 
-            @pl.when(i == 5)
-            def _():
-                for copy in (*inputs(0), *inputs(1)):
-                    copy.start()
+            for k in range(2):
+
+                @pl.when(i == 3 + 3 * k)
+                def _():
+                    for copy in inputs(k):
+                        copy.start()
 
             hidden(i).wait()
             add_to(downs.term(c, 0), t == 0, dot(dytb[:, sliced(t, span)], hidden_at(i)[...]))
@@ -821,21 +831,17 @@
         wides.step3(last - 1, put_wide(last - 1), squares)
         wides.step3(last, put_wide(last), squares)
         out = [move(sums(c), grads_out.at[0, c], g_sem.at[1 + c]) for c in range(chunks)]
+        copies = []
+        for k in range(dm.n - 1, 0, -1):
+            to = lax.rem(me + k, dm.n)
+            copies.append(remote(squares, squares_out.at[me], ssends.at[k - 1], srecvs.at[k - 1], {"dp": to}))
+        copies.append(move(squares, squares_out.at[me], g_sem.at[0]))
+        for copy in copies:
+            copy.start()
         for copy in out:
             copy.start()
-        copies = []
-        for k in range(1, dm.n):
-            to = lax.rem(me + k, dm.n)
-            copies.append(remote(squares, everyone.at[me], ssends.at[k - 1], srecvs.at[k - 1], {"dp": to}))
-        for copy in copies:
-            copy.start()
-        everyone[me] = squares[...]
         for copy in copies:
             copy.wait()
-        total = everyone[0]
-        for k in range(1, dm.n):
-            total = total + everyone[k]
-        total_out[...] = total
         for copy in out:
             copy.wait()
 
@@ -846,8 +852,9 @@
     )
 
 
-def optimizer_kernel(dm, total, grads_in, *refs):
-    ins, outs, (grads, *buffers), (g_sem, in_sem, out_sem) = refs[:9], refs[9:18], refs[18:25], refs[25:]
+def optimizer_kernel(dm, squares_in, grads_in, *refs):
+    ins, outs, (squares, grads, *buffers), (g_sem, in_sem, out_sem) = refs[:9], refs[9:18], refs[18:26], refs[26:]
+    move(squares_in, squares, g_sem.at[dm.layers]).start()
     stores = [buffers[0:2], buffers[2:4], buffers[4:6]]
     halves = 2
     pieces = [(layer, which, half) for layer in range(dm.layers) for which in range(3) for half in range(halves)]
@@ -876,7 +883,11 @@
                 for copy in loads[k]:
                     copy.start()
     count = dm.layers * 3 * dm.d * dm.ff
-    factor = jnp.minimum(1.0, 0.5 * lax.rsqrt(jnp.sum(total[...]) / count + 1e-30))
+    move(squares_in, squares, g_sem.at[dm.layers]).wait()
+    total = squares[0]
+    for k in range(1, dm.n):
+        total = total + squares[k]
+    factor = jnp.minimum(1.0, 0.5 * lax.rsqrt(jnp.sum(total) / count + 1e-30))
     size = dm.d // 2 // dm.n
 
     def adamw(g, refs, at):
@@ -927,7 +938,6 @@
     dm = Dims(w_gate.shape[0], x.shape[0], x.shape[1], w_gate.shape[2], n)
     tokens, d, chunk, chunks, tiles = dm.tokens, dm.d, dm.chunk, dm.chunks, dm.tiles
     hbm = pl.BlockSpec(memory_space=pltpu.HBM)
-    vmem = pl.BlockSpec(memory_space=pltpu.VMEM)
     shape = jax.ShapeDtypeStruct
     dma = lambda *s: pltpu.SemaphoreType.DMA(s)
     natural, turned, per_chunk = (tokens, d), (d, tokens), (chunks, tokens, chunk)
@@ -942,19 +952,19 @@
     def kernel(*refs):
         pl.run_scoped(lambda *scoped: whole_kernel(dm, *refs, *scoped), *semaphores)
 
-    grads, total, *_ = pl.pallas_call(
+    grads, squares, *_ = pl.pallas_call(
         kernel,
         out_shape=[
-            shape((2, chunks, *block), BF), shape((8, LANES), F32), shape(per_chunk, F32), shape(per_chunk, F32), shape(per_chunk, BF),
+            shape((2, chunks, *block), BF), shape((n, 8, LANES), F32), shape(per_chunk, F32), shape(per_chunk, F32), shape(per_chunk, BF),
             shape(turned, BF), shape((chunks - 1, d, chunk), BF), shape(per_chunk, BF), shape(per_chunk, BF),
         ],
         in_specs=[hbm] * 5,
-        out_specs=[hbm, vmem] + [hbm] * 7,
+        out_specs=[hbm] * 9,
         scratch_shapes=[
             pltpu.VMEM(natural, BF), pltpu.VMEM(turned, BF), pltpu.VMEM(turned, BF), pltpu.VMEM(natural, BF), pltpu.VMEM(turned, BF),
             pltpu.VMEM(turned, F32), pltpu.VMEM((chunks + 1, 3, d, chunk), BF), pltpu.VMEM((dm.own_ff, d), BF),
-            pltpu.VMEM((2, 6, *wide), BF), pltpu.VMEM((2, 6, *wide), BF), pltpu.VMEM((chunks, 6, *down), BF), pltpu.VMEM((chunks, 6, *down), BF),
-            pltpu.VMEM((8, LANES), F32), pltpu.VMEM((n, 8, LANES), F32),
+            pltpu.VMEM((2, 6, *wide), BF), pltpu.VMEM((2, 6, *wide), BF), pltpu.VMEM((2, 6, *down), BF), pltpu.VMEM((2, 6, *down), BF),
+            pltpu.VMEM((8, LANES), F32),
         ],
         compiler_params=pltpu.CompilerParams(vmem_limit_bytes=VMEM_LIMIT, collective_id=0, has_side_effects=True),
         name="whole",
@@ -965,16 +975,16 @@
         pl.pallas_call(
             functools.partial(optimizer_kernel, dm),
             out_shape=[shape(w.shape, BF) for w in weights] + [shape(w.shape, F32) for w in weights] * 2,
-            in_specs=[vmem] + [hbm] * 10,
+            in_specs=[hbm] * 11,
             out_specs=[hbm] * 9,
             scratch_shapes=[
-                pltpu.VMEM((2, chunks, *block), BF), pltpu.VMEM(wides, BF), pltpu.VMEM(downs, BF),
+                pltpu.VMEM((n, 8, LANES), F32), pltpu.VMEM((2, chunks, *block), BF), pltpu.VMEM(wides, BF), pltpu.VMEM(downs, BF),
                 pltpu.VMEM(wides, F32), pltpu.VMEM(downs, F32), pltpu.VMEM(wides, F32), pltpu.VMEM(downs, F32),
-                dma(dm.layers), dma(6 * dm.layers, 3), dma(6 * dm.layers, 3),
+                dma(dm.layers + 1), dma(6 * dm.layers, 3), dma(6 * dm.layers, 3),
             ],
             compiler_params=pltpu.CompilerParams(vmem_limit_bytes=VMEM_LIMIT),
             name="optimizer",
-        )(total, grads, *weights, *m, *v)
+        )(squares, grads, *weights, *m, *v)
     )
 
 

time: 280 us -> 271 us (0.968)
  Pallas kernels: 279 us -> 270 us
    pallas_call x1, Pallas kernels: 263 us -> 255 us  [step(): pl.pallas_call(kernel, out_shape=[shape((2, chunks, *block), BF), shape((...]
where the time goes in v4:
time: 271 us
  Pallas kernels  270 us (100%)
    pallas_call x1, Pallas kernels, step(): pl.pallas_call(kernel, out_shape=[shape((2, chunks, *block), BF), shape((...  255 us
    pallas_call x1, Pallas kernels, step(): pl.pallas_call(functools.partial(optimizer_kernel, dm), out_shape=[shape(...  14.7 us

profile of v4, /device:TPU:112, one launch (start us, length us, event | category | flops | bytes accessed | tf_op | source)
XLA Modules:
  0.0 271.0 jit_solution(15797703000997664185)
XLA Ops:
  0.6 255.5 %whole.1 = (bf16[2,4,480,512]{3,2,1,0:T(8,128)(2,1)}, f32[4,8,128]{2,1,0:T(8,128)}, f32[4,4096,512]{2,1,0:T(8,128)}, f32[4,4096,512]{2,1,0:T(8,128)}, bf16[4,409...) custom-call(bf16[4096,640]{1,0:T(8,128)(2,1)} %bitcast.2, ...), custom_call_target="tpu_custom_call" | custom-call | tf_op jit(solution)/shard_map/whole/pallas_call | solution.py:955
  256.1 14.7 %optimizer.1 = (bf16[2,160,2048]{2,1,0:T(8,128)(2,1)}, bf16[2,160,2048]{2,1,0:T(8,128)(2,1)}, bf16[2,512,640]{2,1,0:T(8,128)(2,1)}, f32[2,160,2048]{2,1,0:T(8,12...) custom-call(f32[4,8,128]{2,1,0:T(8,128)} %get-tuple-element.11.squar, ...), custom_call_target="tpu_custom_call" | custom-call | tf_op jit(solution)/shard_map/optimizer/pallas_call | solution.py:975

commit v5 on v4

--- a/solution.py
+++ b/solution.py
@@ -14,7 +14,7 @@
 SMALL = 512
 HALF = 256
 ROWS = 1024
-PIECE = 512
+FEW = 64
 CUT_TILE = 2048
 VMEM_LIMIT = 67043328
 NT = (((1,), (1,)), ((), ()))
@@ -92,6 +92,10 @@
 
 def scale_of(wide, axis, count):
     return lax.rsqrt(jnp.sum(wide * wide, axis, keepdims=True) / count + 1e-6)
+
+
+def down_to_8(x):
+    return jnp.sum(x.reshape(-1, 8, x.shape[-1]), 0)
 
 
 def move(src, dst, sem):
@@ -212,8 +216,8 @@
 
 
 class Scatter:
-    def __init__(self, dm, wide, term, place, slots, send, recv, sends, recvs):
-        self.dm, self.wide, self.term, self.place, self.slots = dm, wide, term, place, slots
+    def __init__(self, dm, wide, terms, place, slots, send, recv, sends, recvs):
+        self.dm, self.wide, self.terms, self.place, self.slots = dm, wide, terms, place, slots
         self.send, self.recv, self.sends, self.recvs = send, recv, sends, recvs
         self.me, self.right, self.left = ring(dm.n)
         self.far = lax.rem(self.me + 2, dm.n)
@@ -226,10 +230,9 @@
     def _parts(self, c, owner, half):
         dm = self.dm
         if self.wide:
-            return [(self.term(c, half)[sliced(owner, dm.rows), :], slice(None))]
-        columns = pl.ds(pl.multiple_of(owner * LANES, LANES), LANES)
-        size = dm.d // 2 // dm.n
-        own = self.term(c, half).at[:, columns]
+            return [(ref[sliced(owner, dm.rows), :], slice(k * HALF, (k + 1) * HALF)) for k, ref in enumerate(self.terms(c, half))]
+        size, per = dm.d // 2 // dm.n, HALF // LANES
+        own = self.terms(c, owner // per).at[:, pl.ds(pl.multiple_of(lax.rem(owner, per) * LANES, LANES), LANES)]
         return [(own[pl.ds(half * (dm.d // 2) + i * size, size), :], slice(i * LANES, (i + 1) * LANES)) for i in range(dm.n)]
 
     def _put(self, c, kind, owner, half, add=None):
@@ -261,7 +264,7 @@
                 g = term.astype(BF)
                 put(half, columns, g)
                 g = g.astype(F32)
-                g = jnp.sum((g * g).reshape(-1, 8, g.shape[-1]), 0)
+                g = down_to_8(g * g)
                 for j in range(0, g.shape[-1], LANES):
                     squares[...] += g[:, j : j + LANES]
         for kind in (2, 3, 4, 5):
@@ -280,8 +283,10 @@
     return (gate * jax.nn.sigmoid(gate) * up).astype(BF)
 
 
-def add_to(ref, first, term):
-    ref[...] = jnp.where(first, 0.0, ref[...]) + term
+def add_to(refs, first, term):
+    for k, ref in enumerate(refs):
+        part = term[:, k * HALF : (k + 1) * HALF]
+        ref[...] = part if first is True else jnp.where(first, 0.0, ref[...]) + part
 
 
 def whole_kernel(
@@ -296,7 +301,7 @@
     gather = Gather(dm, w, gsends, grecvs)
     me, left, right, far = gather.me, gather.left, gather.right, gather.far
     sources = (w_gate, w_up)
-    big_block = lambda i, width: big.at[:, pl.ds(pl.multiple_of(i * width, width), width)]
+    big_blocks = lambda i, width: [big.at[i * (width // HALF) + k] for k in range(width // HALF)]
     saved = [move(w.at[c, 2], wd0.at[c], misc_sem.at[c]) for c in range(chunks - 1)]
     at_last = [move(wd0.at[c], w.at[chunks - 1, c], misc_sem.at[3 + c]) for c in range(chunks - 2)]
     at_end = move(wd0.at[chunks - 2], w.at[chunks, 0], misc_sem.at[5])
@@ -447,11 +452,11 @@
                     ust[slot, rows, part] = up
                     hidden[rows, part] = hidden_of(gate, up)
             if not last:
-                add_to(big.at[:, at_t], c == 0, dot(w[c, 2], hidden[...], NT))
+                add_to(big_blocks(t, TILE), c == 0, dot(w[c, 2], hidden[...], NT))
                 return
             for b in range(0, TILE, HALF):
                 at_b = pl.ds(pl.multiple_of(t * TILE + b, HALF), HALF)
-                total = big[:, at_b] + dot(w[c, 2], hidden[b : b + HALF, :], NT)
+                total = big[t * (TILE // HALF) + b // HALF] + dot(w[c, 2], hidden[b : b + HALF, :], NT)
                 h = xt[:, at_b] + total.astype(BF)
                 wide = h.astype(F32)
                 a = (wide * scale_of(wide, 0, dm.d)).astype(BF)
@@ -495,9 +500,10 @@
 
     def backward1(ba, bg, bu, stash, grads):
         wides = Scatter(
-            dm, True, lambda c, half: big_block(2 * lax.rem(c, 2) + half, dm.chunk), pair, 2, wsend, wrecv, wsends, wrecvs
+            dm, True, lambda c, half: big_blocks(2 * lax.rem(c, 2) + half, dm.chunk), pair, 2, wsend, wrecv, wsends, wrecvs
         )
-        downs = Scatter(dm, False, lambda c, half: big_block(4 + lax.rem(c, 2), dm.chunk), pair, 2, dsend, drecv, dsends, drecvs)
+        down_blocks = lambda c: big_blocks(4 + lax.rem(c, 2), dm.chunk)
+        downs = Scatter(dm, False, lambda c, k: big.at[(4 + lax.rem(c, 2)) * (dm.chunk // HALF) + k], pair, 2, dsend, drecv, dsends, drecvs)
 
         def stored(i):
             slot, chunk, at_t = lax.rem(i, 2), i // tiles, sliced(lax.rem(i, tiles), TILE)
@@ -578,7 +584,7 @@
                 gather.fetched(units - 1, own_sem)
                 gather.step1(units - 1)
 
-            @pl.when(i == 3)
+            @pl.when(i == 4)
             def _():
                 gather.step3(units - 2)
 
@@ -586,7 +592,7 @@
             def _():
                 gather.step2(units - 1)
 
-            @pl.when(i == 7)
+            @pl.when(i == 9)
             def _():
                 gather.step3(units - 1)
 
@@ -620,9 +626,9 @@
                     ba[rows, part] = hidden_of(gate, up)
                     bg[slot, rows, part] = by_gate
                     bu[slot, rows, part] = by_up
-            add_to(wides.term(c, 0), t == 0, dot(at[:, at_t], bg[slot]))
-            add_to(wides.term(c, 1), t == 0, dot(at[:, at_t], bu[slot]))
-            add_to(downs.term(c, 0), t == 0, dot(dytb[:, at_t], ba[...]))
+            add_to(wides.terms(c, 0), t == 0, dot(at[:, at_t], bg[slot]))
+            add_to(wides.terms(c, 1), t == 0, dot(at[:, at_t], bu[slot]))
+            add_to(down_blocks(c), t == 0, dot(dytb[:, at_t], ba[...]))
 
         last = chunks - 1
         for copy in stored(steps - 1):
@@ -642,16 +648,20 @@
             return total.astype(BF)
 
         def finish(t):
-            for k in range(0, SMALL, PIECE):
-                at_k = sliced(t * (SMALL // PIECE) + k // PIECE, PIECE)
-                by_a = stash[:, k : k + PIECE].astype(F32)
-                h = xt[:, at_k].astype(F32)
-                square = jnp.sum(h * h, 0, keepdims=True) / dm.d + 1e-6
+            for k in range(0, SMALL, HALF):
+                at_k = sliced(t * (SMALL // HALF) + k // HALF, HALF)
+                square = along = jnp.zeros((8, HALF), F32)
+                for r in range(0, dm.d, FEW):
+                    by_a, h = stash[r : r + FEW, k : k + HALF].astype(F32), xt[r : r + FEW, at_k].astype(F32)
+                    square, along = square + down_to_8(h * h), along + down_to_8(h * by_a)
+                square = jnp.sum(square, 0, keepdims=True) / dm.d + 1e-6
                 scale = lax.rsqrt(square)
-                along = jnp.sum(h * by_a, 0, keepdims=True) * (scale / square) / dm.d
-                by_h = dytb[:, at_k] + (by_a * scale - h * along).astype(BF)
-                dytb[:, at_k] = by_h
-                abuf[at_k, :] = by_h.T
+                along = jnp.sum(along, 0, keepdims=True) * (scale / square) / dm.d
+                for r in range(0, dm.d, FEW):
+                    by_a, h = stash[r : r + FEW, k : k + HALF].astype(F32), xt[r : r + FEW, at_k].astype(F32)
+                    by_h = dytb[r : r + FEW, at_k] + (by_a * scale - h * along).astype(BF)
+                    dytb[r : r + FEW, at_k] = by_h
+                    abuf[at_k, r : r + FEW] = by_h.T
 
         for copy in inputs(1):
             copy.start()
@@ -690,7 +700,7 @@
             gather.drain(u)
         at_end.start()
         hidden(0).wait()
-        big[:, 0 : dm.chunk] = dot(dytb[:, 0:span], hidden_at(0)[...])
+        add_to(big_blocks(0, dm.chunk), True, dot(dytb[:, 0:span], hidden_at(0)[...]))
         finish(small - 1)
         for neighbour in (left, right):
             pl.semaphore_signal(ready, inc=1, device_id={"dp": neighbour}, device_id_type=pl.DeviceIdType.MESH)
@@ -713,10 +723,10 @@
     def backward0(gb, ub, bg, bu):
         cuts, parts = dm.chunk // HALF, dm.tokens // gb.shape[1]
         wides = Scatter(
-            dm, True, lambda u, half: big_block(2 * chunks * cuts // 2 + 2 * lax.rem(u, 4) + half, HALF), cut, 4, wsend, wrecv, wsends, wrecvs
+            dm, True, lambda u, half: big_blocks(chunks * cuts + 2 * lax.rem(u, 4) + half, HALF), cut, 4, wsend, wrecv, wsends, wrecvs
         )
         downs = Scatter(
-            dm, False, lambda c, half: big_block(c, dm.chunk), spread, chunks, xt.at[:, 0:rest], xt.at[:, rest:], dsends, drecvs
+            dm, False, lambda c, k: big.at[c * cuts + k], spread, chunks, xt.at[:, 0:rest], xt.at[:, rest:], dsends, drecvs
         )
 
         def inputs(i):
@@ -731,27 +741,30 @@
         def _(i):
             c, t = i // 2, lax.rem(i, 2)
 
+            @pl.when(i + 1 < 2 * chunks)
+            def _():
+                hidden(i + 1).start()
+
+            for k in range(4):
+
+                @pl.when(i == 2 + k + k // 2)
+                def _():
+                    inputs(k // 2)[k % 2].start()
+
+            hidden(i).wait()
+            add_to(big_blocks(c, dm.chunk), t == 0, dot(dytb[:, sliced(t, span)], hidden_at(i)[...]))
+
             @pl.when(i == 1)
             def _():
                 pl.semaphore_wait(ready, 2)
 
-            @pl.when(i + 1 < 2 * chunks)
-            def _():
-                hidden(i + 1).start()
-
-            for k in range(2):
-
-                @pl.when(i == 3 + 3 * k)
-                def _():
-                    for copy in inputs(k):
-                        copy.start()
-
-            hidden(i).wait()
-            add_to(downs.term(c, 0), t == 0, dot(dytb[:, sliced(t, span)], hidden_at(i)[...]))
-
             @pl.when(t == 1)
             def _():
                 downs.step1(c)
+
+            @pl.when(jnp.logical_and(t == 1, c >= 2))
+            def _():
+                downs.step2(c - 2)
 
         a0t_back.wait()
         at_end.wait()
@@ -793,13 +806,13 @@
             def _():
                 wides.step2(unit - 2)
 
-            @pl.when(i < chunks)
-            def _():
-                downs.step2(i)
-
-            @pl.when(jnp.logical_and(i >= 2 * chunks, i < 3 * chunks))
-            def _():
-                downs.step3(i - 2 * chunks, put_down(i - 2 * chunks), squares)
+            @pl.when(jnp.logical_and(i >= 1, i < 3))
+            def _():
+                downs.step2(chunks - 3 + i)
+
+            @pl.when(jnp.logical_and(i >= 4, i < 4 + chunks))
+            def _():
+                downs.step3(i - 4, put_down(i - 4), squares)
 
             @pl.when(jnp.logical_and(i >= 1, i + 1 < cut_units * parts))
             def _():
@@ -821,7 +834,7 @@
                     term = dot(at[:, tokens], right[rows, :])
                     totals[k] = term if totals[k] is None else totals[k] + term
             for k in range(2):
-                add_to(wides.term(unit, k), t == 0, totals[k])
+                add_to(wides.terms(unit, k), t == 0, totals[k])
 
         last = cut_units - 1
         wides.step1(last)
@@ -962,7 +975,7 @@
         out_specs=[hbm] * 9,
         scratch_shapes=[
             pltpu.VMEM(natural, BF), pltpu.VMEM(turned, BF), pltpu.VMEM(turned, BF), pltpu.VMEM(natural, BF), pltpu.VMEM(turned, BF),
-            pltpu.VMEM(turned, F32), pltpu.VMEM((chunks + 1, 3, d, chunk), BF), pltpu.VMEM((dm.own_ff, d), BF),
+            pltpu.VMEM((tokens // HALF, d, HALF), F32), pltpu.VMEM((chunks + 1, 3, d, chunk), BF), pltpu.VMEM((dm.own_ff, d), BF),
             pltpu.VMEM((2, 6, *wide), BF), pltpu.VMEM((2, 6, *wide), BF), pltpu.VMEM((2, 6, *down), BF), pltpu.VMEM((2, 6, *down), BF),
             pltpu.VMEM((8, LANES), F32),
         ],

time: 271 us -> 264 us (0.974)
  Pallas kernels: 270 us -> 263 us
    pallas_call x1, Pallas kernels: 255 us -> 249 us  [step(): pl.pallas_call(kernel, out_shape=[shape((2, chunks, *block), BF), shape((...]
where the time goes in v5:
time: 264 us
  Pallas kernels  263 us (100%)
    pallas_call x1, Pallas kernels, step(): pl.pallas_call(kernel, out_shape=[shape((2, chunks, *block), BF), shape((...  249 us
    pallas_call x1, Pallas kernels, step(): pl.pallas_call(functools.partial(optimizer_kernel, dm), out_shape=[shape(...  14.7 us

profile of v5, /device:TPU:112, one launch (start us, length us, event | category | flops | bytes accessed | tf_op | source)
XLA Modules:
  0.0 264.1 jit_solution(7642936659289656765)
XLA Ops:
  0.6 248.6 %whole.1 = (bf16[2,4,480,512]{3,2,1,0:T(8,128)(2,1)}, f32[4,8,128]{2,1,0:T(8,128)}, f32[4,4096,512]{2,1,0:T(8,128)}, f32[4,4096,512]{2,1,0:T(8,128)}, bf16[4,409...) custom-call(bf16[4096,640]{1,0:T(8,128)(2,1)} %bitcast.2, ...), custom_call_target="tpu_custom_call" | custom-call | tf_op jit(solution)/shard_map/whole/pallas_call | solution.py:968
  249.3 14.7 %optimizer.1 = (bf16[2,160,2048]{2,1,0:T(8,128)(2,1)}, bf16[2,160,2048]{2,1,0:T(8,128)(2,1)}, bf16[2,512,640]{2,1,0:T(8,128)(2,1)}, f32[2,160,2048]{2,1,0:T(8,12...) custom-call(f32[4,8,128]{2,1,0:T(8,128)} %get-tuple-element.11.squar, ...), custom_call_target="tpu_custom_call" | custom-call | tf_op jit(solution)/shard_map/optimizer/pallas_call | solution.py:988
